TPU v7x, 32 devices: a whole 2x2x4 slice. The times are simulated.
32 devices in a mesh: grp: 4 (over y, x), dev: 8 (over z, core).
Axes of the slice: x: 2, y: 2, z: 4, core: 2. Of those that a mesh axis runs over, the one named last changes fastest.
Arguments:
- source_id: int32 [524288], P(('grp', 'dev')), may hold values from 0 to 4095, as said below
- slot: int32 [524288], P(('grp', 'dev')), may hold values from 0 to 127, as said below
- owner: int32 [4096], replicated, may hold values from 0 to 4095, as said below
- counts: int32 [4096], P(('grp', 'dev')), may hold values from 1 to 128, as said below
- partials: float32 [5, 524288], P(None, ('grp', 'dev')), may hold values from -6 to 6
- residual: float32 [524288], P(('grp', 'dev')), may hold values from -6 to 6
- weight: float32 [524288], P(('grp', 'dev')), may hold values from 0.3 to 9
- prior: float32 [5, 4096], P(None, ('grp', 'dev')), may hold values from 0.5 to 4
Outputs:
- updates: float32 [5, 4096], P(None, ('grp', 'dev'))
- standardized: float32 [524288], P(('grp', 'dev'))
- norm: float32 [], replicated
Inputs may be any that keep to these rules, and one draw needn't show every extreme that they name: A permutation: source s stands at owner position owner[s], and position p belongs to device p // 128. `source_id`: the rows of one device stand in 32 aligned blocks of 512 rows; block k holds only rows whose source's owner position lies in device k's range. Over all rows, each pair of a source and a slot below 128 appears exactly once. A row is an observation when its slot is below its source's count, else padding. Each device's block of counts holds 128 at least once.
All inputs are finite; a program needn't handle non-finite values.
Results may differ from a plain program's by a relative error of at most 0.0003.
Values sent between devices are 32-bit elements; how exact they have to be, the bound alone decides.
A program may use at most 64 MiB of HBM per device.

v0:
```python
import functools

import jax
import jax.numpy as jnp
from jax import lax
from jax.experimental import pallas as pl
from jax.experimental.pallas import tpu as pltpu
from jax.sharding import PartitionSpec as P

LANES = 128
SUBLANES = 8
UNROLL = 4
MESH = pl.DeviceIdType.MESH


def solve_rows(normal, moments):
    params = len(moments)
    factor = {}
    inverse = []
    for column in range(params):
        running = normal[column][column]
        for earlier in range(column):
            running = running - factor[column, earlier] ** 2
        inverse.append(1.0 / jnp.sqrt(running))
        for target in range(column + 1, params):
            current = normal[target][column]
            for earlier in range(column):
                current = current - factor[target, earlier] * factor[column, earlier]
            factor[target, column] = current * inverse[column]
    forward = []
    for target in range(params):
        current = moments[target]
        for earlier in range(target):
            current = current - factor[target, earlier] * forward[earlier]
        forward.append(current * inverse[target])
    backward = [None] * params
    for target in reversed(range(params)):
        current = forward[target]
        for later in range(target + 1, params):
            current = current - factor[later, target] * backward[later]
        backward[target] = current * inverse[target]
    return backward


def thirds(values):
    high = values.astype(jnp.bfloat16).astype(jnp.float32)
    rest = values - high
    middle = rest.astype(jnp.bfloat16).astype(jnp.float32)
    return [high, middle, rest - middle]


def stacked(values, rows):
    terms = thirds(values)
    spare = rows - 3 * values.shape[0]
    if spare:
        terms.append(jnp.zeros((spare, values.shape[1]), jnp.float32))
    return jnp.concatenate(terms, axis=0).astype(jnp.bfloat16)


def kernel(
    sizes,
    source_hbm, slot_hbm, owner_hbm, counts_hbm, partials_hbm, residual_hbm, weight_hbm, prior_hbm,
    updates_ref, fresh_ref, norm_ref,
    source_ref, slot_ref, owner_ref, counts_ref, partials_ref, residual_ref, weight_ref, prior_ref,
    out_buf, in_buf, hot_buf, back_out, back_in, tail_out, tail_in,
    load_sem, tail_send_sem, tail_recv_sem, send_sem, recv_sem, back_send_sem, back_recv_sem,
):
    n, members, width, pad_slots = sizes
    params = partials_ref.shape[0]
    words = params + 2
    half = members // 2
    side = n // 2
    groups = n // members
    row_pairs = (
        (owner_hbm, owner_ref), (weight_hbm, weight_ref), (partials_hbm, partials_ref),
        (residual_hbm, residual_ref), (source_hbm, source_ref), (slot_hbm, slot_ref),
        (counts_hbm, counts_ref), (prior_hbm, prior_ref),
    )
    loads = [pltpu.make_async_copy(a, b, load_sem.at[i]) for i, (a, b) in enumerate(row_pairs)]
    for load in loads:
        load.start()
    src_local = counts_ref.shape[1]
    my_group, my_member = lax.axis_index("grp"), lax.axis_index("dev")
    me = my_group * members + my_member

    def target(i, far):
        group = (my_group + i // half) % groups
        member = (my_member // half + far) % 2 * half + (my_member % half + i % half) % half
        return group * members + member

    def origin(i, far):
        group = (my_group + groups - i // half) % groups
        member = (my_member // half + far) % 2 * half + (my_member % half + half - i % half) % half
        return group * members + member

    def coords(device):
        return (device // members, device % members)

    barrier = pltpu.get_barrier_semaphore()

    def greet(step, carry):
        peer = (me + step) % n
        pl.semaphore_signal(barrier, inc=1, device_id=coords(peer), device_id_type=MESH)
        return carry

    lax.fori_loop(1, n, greet, 0)

    for load in loads:
        load.wait()
    def prepare(step, carry):
        for part in range(UNROLL):
            k = step * UNROLL + part
            cols = pl.ds(pl.multiple_of(k * width, LANES), width)
            root = jnp.sqrt(weight_ref[:, cols])
            out_buf[k, 0:params, :] = partials_ref[:, cols] * root
            out_buf[k, params : params + 1, :] = residual_ref[:, cols] * root
            cell = source_ref[:, cols] * pad_slots + slot_ref[:, cols]
            out_buf[k, params + 1 : words, :] = cell.astype(jnp.float32)
            in_buf[k, words:SUBLANES, :] = jnp.zeros((SUBLANES - words, width), jnp.float32)
        return carry

    lax.fori_loop(0, n // UNROLL, prepare, 0)

    pl.semaphore_wait(barrier, n - 1)

    def forward(peer, slot):
        return pltpu.make_async_remote_copy(
            src_ref=out_buf.at[peer, pl.ds(0, words)],
            dst_ref=in_buf.at[slot, pl.ds(0, words)],
            send_sem=send_sem,
            recv_sem=recv_sem.at[slot],
            device_id=coords(peer),
            device_id_type=MESH,
        )

    forward(target(0, 1), me).start()

    def send(step, carry):
        forward(target(step, 1), me).start()
        forward(target(step, 0), me).start()
        return carry

    lax.fori_loop(1, side, send, 0)

    position = me * src_local + lax.broadcasted_iota(jnp.int32, (src_local, LANES), 0)

    def invert(tile, total):
        ids = tile * LANES + lax.broadcasted_iota(jnp.int32, (1, LANES), 1)
        return total + jnp.where(owner_ref[pl.ds(tile, 1), :] == position, ids, 0)

    found = lax.fori_loop(0, owner_ref.shape[0], invert, jnp.zeros((src_local, LANES), jnp.int32))
    source_at = jnp.sum(found.astype(jnp.float32), axis=1, keepdims=True)
    counts = counts_ref[...].astype(jnp.float32)
    diagonal = lax.broadcasted_iota(jnp.int32, (src_local, src_local), 0) == lax.broadcasted_iota(
        jnp.int32, (src_local, src_local), 1
    )
    count_column = jnp.sum(jnp.where(diagonal, counts, 0.0), axis=1, keepdims=True)
    first_cell = source_at * pad_slots
    end_cell = first_cell + count_column

    def absorb(k):
        rows = in_buf[k, 0:words, :]
        cell = rows[params + 1 : params + 2, :]
        hit = jnp.logical_and(cell >= first_cell, cell < end_cell)
        hot = jnp.where(hit, 1.0, 0.0).astype(jnp.bfloat16)
        hot_buf[k] = hot
        products = []
        for i in range(params):
            products.append(rows[i : i + 1, :] * in_buf[k])
        return lax.dot_general(
            stacked(jnp.concatenate(products, axis=0), LANES), hot, (((1,), (1,)), ((), ())),
            preferred_element_type=jnp.float32,
        )

    in_buf[me, 0:words, :] = out_buf[me, 0:words, :]
    far = origin(0, 1)
    forward(far, far).wait_recv()
    total = absorb(me) + absorb(far)

    def arrive(step, total):
        near, far = origin(step, 0), origin(step, 1)
        forward(near, near).wait_recv()
        forward(far, far).wait_recv()
        return total + absorb(near) + absorb(far)

    total = lax.fori_loop(1, side, arrive, total)

    height = params * SUBLANES
    sums = total[0:height] + total[height : 2 * height] + total[2 * height : 3 * height]
    normal = [[None] * params for _ in range(params)]
    for i in range(params):
        for j in range(i, params):
            entry = sums[i * SUBLANES + j : i * SUBLANES + j + 1]
            if i == j:
                entry = entry + prior_ref[i : i + 1, :]
            normal[i][j] = entry
            normal[j][i] = entry
    moments = [sums[i * SUBLANES + params : i * SUBLANES + params + 1] for i in range(params)]
    updates = solve_rows(normal, moments)
    for i in range(params):
        updates_ref[i : i + 1, :] = updates[i]
    blank = jnp.zeros((1, src_local), jnp.float32)
    table = jnp.concatenate(updates + [blank - 1.0] + [blank] * (SUBLANES - params - 1), axis=0)
    table = stacked(table, 4 * SUBLANES)

    def backward(peer, slot):
        return pltpu.make_async_remote_copy(
            src_ref=back_out.at[peer],
            dst_ref=back_in.at[slot],
            send_sem=back_send_sem,
            recv_sem=back_recv_sem,
            device_id=coords(peer),
            device_id_type=MESH,
        )

    def summary(peer, slot):
        return pltpu.make_async_remote_copy(
            src_ref=tail_out,
            dst_ref=tail_in.at[slot],
            send_sem=tail_send_sem,
            recv_sem=tail_recv_sem,
            device_id=coords(peer),
            device_id_type=MESH,
        )

    def refit(k):
        spread = jnp.dot(table, hot_buf[k], preferred_element_type=jnp.float32)
        spread = spread[0:SUBLANES] + spread[SUBLANES : 2 * SUBLANES] + spread[2 * SUBLANES : 3 * SUBLANES]
        fresh = -jnp.sum(in_buf[k] * spread, axis=0, keepdims=True)
        back_out[k, :, 0:width] = fresh
        return fresh * fresh

    def refit_far(step, squares):
        for part in range(UNROLL):
            squares = squares + refit(target(step * UNROLL + part, 1))
        return squares

    def refit_near(step, squares):
        for part in range(UNROLL):
            squares = squares + refit(target(step * UNROLL + part, 0))
        return squares

    squares = lax.fori_loop(0, side // UNROLL, refit_far, jnp.zeros((1, width), jnp.float32))
    squares = lax.fori_loop(0, side // UNROLL, refit_near, squares)
    lane = lax.broadcasted_iota(jnp.int32, (1, LANES), 1)
    square_sum = jnp.sum(squares, axis=1, keepdims=True)
    count_sum = jnp.sum(counts, axis=1, keepdims=True)
    tail_out[...] = jnp.where(lane == 0, square_sum, jnp.where(lane == 1, count_sum, 0.0))

    def finish(step, carry):
        for part in range(UNROLL):
            back_out[step * UNROLL + part, :, width : width + LANES] = tail_out[...]
        return carry

    lax.fori_loop(0, n // UNROLL, finish, 0)

    def send_far_tail(step, carry):
        backward(target(step, 1), me).start()
        return carry

    def send_near(step, carry):
        backward(target(step, 0), me).start()
        return carry

    lax.fori_loop(0, side, send_far_tail, 0)
    lax.fori_loop(1, side, send_near, 0)
    back_in[me] = back_out[me]

    others = pl.ds(0, n - 1)
    for ref, semaphore in ((back_in.at[others], back_recv_sem),):
        pltpu.make_async_remote_copy(
            src_ref=ref,
            dst_ref=ref,
            send_sem=back_send_sem,
            recv_sem=semaphore,
            device_id=coords((me + 1) % n),
            device_id_type=MESH,
        ).wait_recv()

    def gather_tails(k, tails):
        return tails + back_in[k, :, width : width + LANES]

    tails = lax.fori_loop(0, n, gather_tails, jnp.zeros((1, LANES), jnp.float32))
    square_total = jnp.sum(jnp.where(lane == 0, tails, 0.0), axis=1, keepdims=True)
    count_total = jnp.sum(jnp.where(lane == 1, tails, 0.0), axis=1, keepdims=True)
    norm = jnp.sqrt(square_total / count_total + 1e-06)
    norm_ref[...] = jnp.broadcast_to(norm, norm_ref.shape)
    scale = 1.0 / norm

    def emit(step, carry):
        for part in range(UNROLL):
            k = step * UNROLL + part
            cols = pl.ds(pl.multiple_of(k * width, LANES), width)
            fresh_ref[:, cols] = back_in[k, :, 0:width] * scale
        return carry

    lax.fori_loop(0, n // UNROLL, emit, 0)

    sent = (out_buf.at[pl.ds(0, n - 1), pl.ds(0, words)], back_out.at[pl.ds(0, n - 1)])
    for ref, semaphore in zip(sent, (send_sem, back_send_sem)):
        pltpu.make_async_remote_copy(
            src_ref=ref,
            dst_ref=ref,
            send_sem=semaphore,
            recv_sem=recv_sem.at[me],
            device_id=coords((me + 1) % n),
            device_id_type=MESH,
        ).wait_send()


def release(a_ref, b_ref, c_ref, a_out, b_out, c_out, sem):
    pairs = ((a_ref, a_out), (b_ref, b_out), (c_ref, c_out))
    copies = [pltpu.make_async_copy(x, y, sem.at[i]) for i, (x, y) in enumerate(pairs)]
    for copy in copies:
        copy.start()
    for copy in copies:
        copy.wait()


def body(source_id, slot, owner, counts, partials, residual, weight, prior):
    members = lax.axis_size("dev")
    n = lax.axis_size("grp") * members
    params = partials.shape[0]
    row_count = residual.shape[0]
    src_local = counts.shape[0]
    block_rows = row_count // n
    width = -(-block_rows // LANES) * LANES

    def lay(array, fill):
        array = array.reshape(-1, row_count)
        if width == block_rows:
            return array
        blocks = array.reshape(-1, n, block_rows)
        blocks = jnp.pad(blocks, ((0, 0), (0, 0), (0, width - block_rows)), constant_values=fill)
        return blocks.reshape(-1, n * width)

    vmem = pl.BlockSpec(memory_space=pltpu.VMEM)
    operands = (
        lay(source_id, -1),
        lay(slot, 0),
        owner.reshape(-1, LANES),
        counts.reshape(1, src_local),
        lay(partials, 0),
        lay(residual, 0),
        lay(weight, 1),
        prior,
    )
    updates, standardized, norm = pl.pallas_call(
        functools.partial(kernel, (n, members, width, row_count // src_local)),
        out_shape=(
            jax.ShapeDtypeStruct((params, src_local), jnp.float32),
            jax.ShapeDtypeStruct((1, n * width), jnp.float32),
            jax.ShapeDtypeStruct((1, LANES), jnp.float32),
        ),
        in_specs=[pl.BlockSpec(memory_space=pltpu.HBM)] * len(operands),
        out_specs=(vmem, vmem, vmem),
        scratch_shapes=[pltpu.VMEM(operand.shape, operand.dtype) for operand in operands] + [
            pltpu.VMEM((n, SUBLANES, width), jnp.float32),
            pltpu.VMEM((n, SUBLANES, width), jnp.float32),
            pltpu.VMEM((n, src_local, width), jnp.bfloat16),
            pltpu.VMEM((n, 1, width + LANES), jnp.float32),
            pltpu.VMEM((n, 1, width + LANES), jnp.float32),
            pltpu.VMEM((1, LANES), jnp.float32),
            pltpu.VMEM((n, 1, LANES), jnp.float32),
            pltpu.SemaphoreType.DMA((len(operands),)),
            pltpu.SemaphoreType.DMA,
            pltpu.SemaphoreType.DMA,
            pltpu.SemaphoreType.DMA,
            pltpu.SemaphoreType.DMA((n,)),
            pltpu.SemaphoreType.DMA,
            pltpu.SemaphoreType.DMA,
        ],
        compiler_params=pltpu.CompilerParams(
            collective_id=0, has_side_effects=True, vmem_limit_bytes=65000 * 1024
        ),
        name="exchange_fit",
    )(*operands)
    results = (updates, standardized, norm)
    updates, standardized, norm = pl.pallas_call(
        release,
        out_shape=tuple(jax.ShapeDtypeStruct(r.shape, r.dtype) for r in results),
        in_specs=[vmem] * 3,
        out_specs=[pl.BlockSpec(memory_space=pltpu.HBM)] * 3,
        scratch_shapes=[pltpu.SemaphoreType.DMA((3,))],
        name="release",
    )(*results)
    standardized = standardized.reshape(n, width)[:, :block_rows] if width != block_rows else standardized
    return (updates, standardized.reshape(row_count), norm[0, 0])


def solution(mesh):
    in_specs = (
        P(("grp", "dev")),
        P(("grp", "dev")),
        P(),
        P(("grp", "dev")),
        P(None, ("grp", "dev")),
        P(("grp", "dev")),
        P(("grp", "dev")),
        P(None, ("grp", "dev")),
    )
    out_specs = (P(None, ("grp", "dev")), P(("grp", "dev")), P())
    return jax.shard_map(body, mesh=mesh, in_specs=in_specs, out_specs=out_specs, check_vma=False)
```

profile of v0, /device:TPU:0, one launch (start us, length us, event | category | flops | bytes accessed | tf_op | source)
XLA Modules:
  0.0 30.7 jit_solution(6889202244856008317)
XLA Ops:
  0.6 28.5 %exchange_fit.1 = (f32[5,128]{1,0:T(8,128)}, f32[1,16384]{1,0:T(1,128)}, f32[1,128]{1,0:T(1,128)}) custom-call(s32[1,16384]{1,0:T(1,128)} %bitcast.9, s32[1,16384]{1,0:T(1,128)} %bitcast.10, s32[32,128]{1,0:T(8,128)} %bitcast.13, s32[1,128]{1,0:T(1,128)} %bitcast.14, f32[5,16384]{1,0:T(8,128)} %partials_hbm.1, f32[1,16384]{1,0:T(1,128)} %bitcast.11, ...), custom_call_target="tpu_custom_call" | custom-call | tf_op jit(solution)/shard_map/exchange_fit/pallas_call | solution.py:348
  29.1 1.5 %release.1 = (f32[5,128]{1,0:T(8,128)}, f32[1,16384]{1,0:T(1,128)}, f32[1,128]{1,0:T(1,128)}) custom-call(f32[5,128]{1,0:T(8,128)} %get-tuple-element.9.a_ref, f32[1,16384]{1,0:T(1,128)} %get-tuple-element.10.b_ref, f32[1,128]{1,0:T(1,128)} %get-tuple-element.11.c_ref), custom_call_target="tpu_custom_call" | custom-call | tf_op jit(solution)/shard_map/release/pallas_call | solution.py:379
where the time goes:
time: 30.9 us; the launch traced here: 30.7 us
  Pallas kernels  30 us (97%)
  between operations  0.64 us (2%)
    pallas_call x1, Pallas kernels, body(): pl.pallas_call(functools.partial(kernel, (n, members, width, row_count //...  28.5 us
    pallas_call x1, Pallas kernels, body(): pl.pallas_call(release, out_shape=tuple((jax.ShapeDtypeStruct(r.shape, r....  1.5 us

commit v1 on v0

v1 whole, which is shorter than its diff:
```python
import functools

import jax
import jax.numpy as jnp
from jax import lax
from jax.experimental import pallas as pl
from jax.experimental.pallas import tpu as pltpu
from jax.sharding import PartitionSpec as P

LANES = 128
SUBLANES = 8
CORES = 2
MESH = pl.DeviceIdType.MESH


def solve_rows(normal, moments):
    params = len(moments)
    factor = {}
    inverse = []
    for column in range(params):
        running = normal[column][column]
        for earlier in range(column):
            running = running - factor[column, earlier] ** 2
        inverse.append(1.0 / jnp.sqrt(running))
        for target in range(column + 1, params):
            current = normal[target][column]
            for earlier in range(column):
                current = current - factor[target, earlier] * factor[column, earlier]
            factor[target, column] = current * inverse[column]
    forward = []
    for target in range(params):
        current = moments[target]
        for earlier in range(target):
            current = current - factor[target, earlier] * forward[earlier]
        forward.append(current * inverse[target])
    backward = [None] * params
    for target in reversed(range(params)):
        current = forward[target]
        for later in range(target + 1, params):
            current = current - factor[later, target] * backward[later]
        backward[target] = current * inverse[target]
    return backward


def thirds(values):
    high = values.astype(jnp.bfloat16).astype(jnp.float32)
    rest = values - high
    middle = rest.astype(jnp.bfloat16).astype(jnp.float32)
    return jnp.concatenate([high, middle, rest - middle], axis=0).astype(jnp.bfloat16)


def gather_lanes(table, index):
    return jnp.take_along_axis(table, index, axis=1, mode="promise_in_bounds")


def kernel(
    sizes,
    source_hbm, slot_hbm, owner_hbm, counts_hbm, partials_hbm, residual_hbm, weight_hbm, prior_hbm,
    updates_ref, fresh_ref, norm_ref,
    source_ref, slot_ref, owner_ref, counts_ref, partials_ref, residual_ref, weight_ref, prior_ref,
    root_buf, cell_buf, place_buf, out_buf, in_buf, meta_buf, ends_buf, sums_buf, tables,
    load_sem, send_sem, recv_sem, meta_send_sem, meta_recv_sem, sums_send_sem, sums_recv_sem,
    table_send_sem, table_recv_sem,
):
    groups, members, width, pad_slots = sizes
    n = groups * members
    params = partials_ref.shape[0]
    words = params + 2
    items = params + 1
    depth = members // CORES
    plane = groups * CORES
    pieces = width // LANES
    low = 2 if groups % 2 == 0 else 1
    high = groups // low
    row_pairs = (
        (owner_hbm, owner_ref), (source_hbm, source_ref), (slot_hbm, slot_ref), (weight_hbm, weight_ref),
        (residual_hbm, residual_ref), (partials_hbm, partials_ref), (counts_hbm, counts_ref), (prior_hbm, prior_ref),
    )
    loads = [pltpu.make_async_copy(a, b, load_sem.at[i]) for i, (a, b) in enumerate(row_pairs)]
    for load in loads:
        load.start()
    my_group, my_member = lax.axis_index("grp"), lax.axis_index("dev")
    my_depth, my_core = my_member // CORES, my_member % CORES
    me = my_group * members + my_member
    my_seat = my_group * CORES + my_core

    def target(step):
        jump = step // CORES
        group = (my_group // low + jump // low) % high * low + (my_group % low + jump % low) % low
        return group, (my_core + step % CORES) % CORES

    def origin(step):
        jump = step // CORES
        group = (my_group // low + high - jump // low) % high * low + (my_group % low + low - jump % low) % low
        return group, (my_core + CORES - step % CORES) % CORES

    def seat_coords(seat):
        group, core = seat
        return (group, my_depth * CORES + core)

    def level_coords(level):
        return (my_group, level * CORES + my_core)

    barrier = pltpu.get_barrier_semaphore()

    def greet(step, carry):
        pl.semaphore_signal(barrier, inc=1, device_id=seat_coords(target(step)), device_id_type=MESH)
        return carry

    def greet_level(step, carry):
        pl.semaphore_signal(barrier, inc=1, device_id=level_coords((my_depth + step) % depth), device_id_type=MESH)
        return carry

    lax.fori_loop(1, depth, greet_level, 0)
    lax.fori_loop(1, plane, greet, 0)

    for load in loads:
        load.wait()

    meta_buf[my_depth] = jnp.concatenate(
        [prior_ref[...], counts_ref[...].astype(jnp.float32), jnp.zeros((SUBLANES - items, LANES), jnp.float32)], axis=0
    )
    batch = min(32, owner_ref.shape[0])

    def locate(step, carry):
        rows = pl.ds(pl.multiple_of(step * SUBLANES, SUBLANES), SUBLANES)
        source = source_ref[rows, :]
        lane, tile = source % LANES, source // LANES

        def look(group, found):
            for t in range(batch):
                row = group * batch + t
                entry = jnp.broadcast_to(owner_ref[pl.ds(row, 1), :], (SUBLANES, LANES))
                found = jnp.where(tile == row, gather_lanes(entry, lane), found)
            return found

        found = jnp.full((SUBLANES, LANES), -1, jnp.int32)
        if owner_ref.shape[0] == batch:
            found = look(0, found)
        else:
            found = lax.fori_loop(0, owner_ref.shape[0] // batch, look, found)
        place = found % LANES
        place_buf[rows, :] = place
        cell = jnp.where(found < 0, -1, place * pad_slots + slot_ref[rows, :])
        cell_buf[rows, :] = cell.astype(jnp.float32)
        root = jnp.sqrt(weight_ref[rows, :])
        root_buf[rows, :] = root
        residual_ref[rows, :] = residual_ref[rows, :] * root
        return carry

    lax.fori_loop(0, source_ref.shape[0] // SUBLANES, locate, 0)

    sublane = lax.broadcasted_iota(jnp.int32, (SUBLANES, LANES), 0)

    def prepare(k, carry):
        for piece in range(pieces):
            row = pl.ds(k * pieces + piece, 1)
            cols = pl.ds(pl.multiple_of(k * width + piece * LANES, LANES), LANES)

            def spread(ref):
                return jnp.broadcast_to(ref[row, :], (SUBLANES, LANES))

            scaled = partials_ref[:, cols] * jnp.broadcast_to(root_buf[row, :], (params, LANES))
            part = slice(piece * LANES, (piece + 1) * LANES)
            out_buf[k, 0:params, part] = scaled
            out_buf[k, params:items, part] = residual_ref[row, :]
            out_buf[k, items:words, part] = cell_buf[row, :]
            out_buf[k, words : words + 1, part] = slot_ref[row, :].astype(jnp.float32)
        return carry

    lax.fori_loop(0, n, prepare, 0)

    pl.semaphore_wait(barrier, plane - 1 + depth - 1)

    def meta_copy(level, slot):
        return pltpu.make_async_remote_copy(
            src_ref=meta_buf.at[slot], dst_ref=meta_buf.at[slot], send_sem=meta_send_sem, recv_sem=meta_recv_sem,
            device_id=level_coords(level), device_id_type=MESH,
        )

    def row_copy(level, seat, slot):
        group, core = seat
        return pltpu.make_async_remote_copy(
            src_ref=out_buf.at[group * members + level * CORES + core, pl.ds(0, words)],
            dst_ref=in_buf.at[level, slot, pl.ds(0, words)],
            send_sem=send_sem, recv_sem=recv_sem.at[level, slot],
            device_id=seat_coords(seat), device_id_type=MESH,
        )

    def sums_copy(level, stage, slot):
        return pltpu.make_async_remote_copy(
            src_ref=sums_buf.at[slot, stage], dst_ref=sums_buf.at[slot, stage],
            send_sem=sums_send_sem, recv_sem=sums_recv_sem.at[stage, slot],
            device_id=level_coords(level), device_id_type=MESH,
        )

    def table_copy(stage, seat, slot):
        return pltpu.make_async_remote_copy(
            src_ref=tables.at[slot], dst_ref=tables.at[slot],
            send_sem=table_send_sem, recv_sem=table_recv_sem.at[stage],
            device_id=seat_coords(seat), device_id_type=MESH,
        )

    def send_meta(step, carry):
        meta_copy((my_depth + step) % depth, my_depth).start()
        return carry

    lax.fori_loop(1, depth, send_meta, 0)

    def send_rows(level, carry):
        def send_one(step, carry):
            row_copy(level, target(plane - 1 - step), my_seat).start()
            return carry

        return lax.fori_loop(0, plane - 1, send_one, carry)

    lax.fori_loop(0, depth, send_rows, 0)

    def own_rows(level, carry):
        in_buf[level, my_seat] = out_buf[my_group * members + level * CORES + my_core]
        return carry

    lax.fori_loop(0, depth, own_rows, 0)

    others = pl.ds(0, depth - 1)
    pltpu.make_async_remote_copy(
        src_ref=meta_buf.at[others], dst_ref=meta_buf.at[others], send_sem=meta_send_sem, recv_sem=meta_recv_sem,
        device_id=level_coords((my_depth + 1) % depth), device_id_type=MESH,
    ).wait_recv()

    src_local = counts_ref.shape[1]
    square = (src_local, LANES)
    first_cell = lax.broadcasted_iota(jnp.int32, square, 0) * pad_slots
    diagonal = lax.broadcasted_iota(jnp.int32, square, 0) == lax.broadcasted_iota(jnp.int32, square, 1)
    first_cell = first_cell.astype(jnp.float32)

    def find_ends(level, carry):
        counts = meta_buf[level, params:items, :]
        column = jnp.sum(jnp.where(diagonal, counts, 0.0), axis=1, keepdims=True)
        ends_buf[level] = first_cell + column
        return carry

    lax.fori_loop(0, depth, find_ends, 0)
    wide_sublane = lax.broadcasted_iota(jnp.int32, (SUBLANES, width), 0)

    def absorb(level, slot):
        rows = in_buf[level, slot]
        cell = rows[items:words, :]
        rows = jnp.where(wide_sublane < items, rows, 0.0)
        end_cell = ends_buf[level]
        hot = []
        for piece in range(pieces):
            part = cell[:, piece * LANES : (piece + 1) * LANES]
            hit = jnp.logical_and(part >= first_cell, part < end_cell)
            hot.append(jnp.where(hit, 1.0, 0.0))
        hot = jnp.concatenate(hot, axis=1).astype(jnp.bfloat16)
        products = jnp.concatenate([rows[i : i + 1, :] * rows for i in range(items)], axis=0)
        return lax.dot_general(
            thirds(products), hot, (((1,), (1,)), ((), ())), preferred_element_type=jnp.float32
        )

    height = items * SUBLANES

    def gather_level(level, carry):
        total = absorb(level, my_seat)

        def arrive(step, total):
            group, core = origin(plane - 1 - step)
            seat = (group, core)
            slot = group * CORES + core
            row_copy(level, seat, slot).wait_recv()
            return total + absorb(level, slot)

        total = lax.fori_loop(0, plane - 1, arrive, total)
        total = total[0:height] + total[height : 2 * height] + total[2 * height : 3 * height]
        blocks = [total[i * SUBLANES : (i + 1) * SUBLANES] for i in range(items)]
        first = jnp.where(sublane == items, pltpu.roll(blocks[5], 1, 0), blocks[0])
        second = jnp.where(
            jnp.logical_or(sublane == 0, sublane >= items), pltpu.roll(blocks[3], 3, 0), blocks[1]
        )
        third = jnp.where(sublane < 2, pltpu.roll(blocks[4], 4, 0), blocks[2])
        sums_buf[my_depth, level] = jnp.concatenate([first, second, third], axis=0)

        def send_sums(step, carry):
            sums_copy((my_depth + step) % depth, level, my_depth).start()
            return carry

        lax.fori_loop(1, depth, send_sums, 0)
        return carry

    lax.fori_loop(0, depth, gather_level, 0)

    at = {(0, 0): 0, (0, 1): 1, (0, 2): 2, (0, 3): 3, (0, 4): 4, (0, 5): 5, (5, 5): 6,
          (3, 5): 8, (1, 1): 9, (1, 2): 10, (1, 3): 11, (1, 4): 12, (1, 5): 13, (3, 3): 14, (3, 4): 15,
          (4, 4): 16, (4, 5): 17, (2, 2): 18, (2, 3): 19, (2, 4): 20, (2, 5): 21}

    def fit_level(level, carry):
        def fetch(step, carry):
            other = (my_depth + depth - step) % depth
            sums_copy(other, level, other).wait_recv()
            return carry

        lax.fori_loop(1, depth, fetch, 0)

        def gather_sums(slot, total):
            return total + sums_buf[slot, level]

        total = lax.fori_loop(1, depth, gather_sums, sums_buf[0, level])

        def entry(i, j):
            spot = at[min(i, j), max(i, j)]
            return total[spot : spot + 1, :]

        normal = [[entry(i, j) for j in range(params)] for i in range(params)]
        moments = [entry(i, params) for i in range(params)]
        with_prior = [[normal[i][j] for j in range(params)] for i in range(params)]
        for i in range(params):
            with_prior[i][i] = normal[i][i] + meta_buf[level, i : i + 1, :]
        updates = solve_rows(with_prior, moments)
        squares = entry(params, params)
        for i in range(params):
            fitted = normal[i][0] * updates[0]
            for j in range(1, params):
                fitted = fitted + normal[i][j] * updates[j]
            squares = squares + updates[i] * (fitted - 2.0 * moments[i])
        counts = meta_buf[level, params:items, :]
        mine = my_group * members + level * CORES + my_core
        tables[mine] = jnp.concatenate(updates + [jnp.full((1, LANES), -1.0, jnp.float32), squares, counts], axis=0)

        def send_table(step, carry):
            table_copy(level, target(plane - 1 - step), mine).start()
            return carry

        lax.fori_loop(0, plane - 1, send_table, 0)
        return carry

    lax.fori_loop(0, depth, fit_level, 0)
    updates_ref[...] = tables[me, 0:params, :]

    def refit_level(level, carry):
        seats = pl.ds(0, plane - 1)
        pltpu.make_async_remote_copy(
            src_ref=tables.at[seats], dst_ref=tables.at[seats],
            send_sem=table_send_sem, recv_sem=table_recv_sem.at[level],
            device_id=seat_coords(target(1)), device_id_type=MESH,
        ).wait_recv()

        def refit(seat, carry):
            k = seat // CORES * members + level * CORES + seat % CORES
            table = tables[k]
            for piece in range(pieces):
                row = pl.ds(k * pieces + piece, 1)
                place = jnp.broadcast_to(place_buf[row, :], (SUBLANES, LANES))
                picked = gather_lanes(table, place)
                rows = out_buf[k, :, piece * LANES : (piece + 1) * LANES]
                fresh = -jnp.sum(jnp.where(sublane < items, picked * rows, 0.0), axis=0, keepdims=True)
                live = rows[words : words + 1, :] < picked[words : words + 1, :]
                root_buf[row, :] = jnp.where(live, fresh, 0.0)
            return carry

        return lax.fori_loop(0, plane, refit, carry)

    lax.fori_loop(0, depth, refit_level, 0)

    def tally(k, tails):
        return tails + tables[k, items : words + 1, :]

    tails = lax.fori_loop(0, n, tally, jnp.zeros((2, LANES), jnp.float32))
    tails = jnp.sum(tails, axis=1, keepdims=True)
    norm = jnp.sqrt(jnp.maximum(tails[0:1], 0.0) / tails[1:2] + 1e-06)
    norm_ref[...] = jnp.broadcast_to(norm, norm_ref.shape)
    scale = 1.0 / norm
    fresh_ref[...] = root_buf[...] * scale

    def drain(ref, semaphore):
        pltpu.make_async_remote_copy(
            src_ref=ref, dst_ref=ref, send_sem=semaphore, recv_sem=meta_recv_sem,
            device_id=seat_coords(target(1)), device_id_type=MESH,
        ).wait_send()

    sent = depth * (plane - 1)
    drain(out_buf.at[pl.ds(0, sent), pl.ds(0, words)], send_sem)
    drain(meta_buf.at[others], meta_send_sem)
    drain(sums_buf.at[others], sums_send_sem)
    drain(tables.at[pl.ds(0, sent)], table_send_sem)


def release(a_ref, b_ref, c_ref, a_out, b_out, c_out, sem):
    pairs = ((a_ref, a_out), (b_ref, b_out), (c_ref, c_out))
    copies = [pltpu.make_async_copy(x, y, sem.at[i]) for i, (x, y) in enumerate(pairs)]
    for copy in copies:
        copy.start()
    for copy in copies:
        copy.wait()


def body(source_id, slot, owner, counts, partials, residual, weight, prior):
    groups, members = lax.axis_size("grp"), lax.axis_size("dev")
    n = groups * members
    params = partials.shape[0]
    row_count = residual.shape[0]
    src_local = counts.shape[0]
    block_rows = row_count // n
    width = -(-block_rows // LANES) * LANES
    depth, plane = members // CORES, groups * CORES

    def lay(array, fill):
        if width == block_rows:
            return array
        blocks = array.reshape(-1, n, block_rows)
        blocks = jnp.pad(blocks, ((0, 0), (0, 0), (0, width - block_rows)), constant_values=fill)
        return blocks.reshape(array.shape[:-1] + (n * width,))

    def dense(array, fill):
        return lay(array, fill).reshape(-1, LANES)

    vmem = pl.BlockSpec(memory_space=pltpu.VMEM)
    operands = (
        dense(source_id, -1),
        dense(slot, 0),
        owner.reshape(-1, LANES),
        counts.reshape(1, src_local),
        lay(partials, 0),
        dense(residual, 0),
        dense(weight, 1),
        prior,
    )
    rows = n * width // LANES
    updates, standardized, norm = pl.pallas_call(
        functools.partial(kernel, (groups, members, width, row_count // src_local)),
        out_shape=(
            jax.ShapeDtypeStruct((params, src_local), jnp.float32),
            jax.ShapeDtypeStruct((rows, LANES), jnp.float32),
            jax.ShapeDtypeStruct((1, LANES), jnp.float32),
        ),
        in_specs=[pl.BlockSpec(memory_space=pltpu.HBM)] * len(operands),
        out_specs=(vmem, vmem, vmem),
        scratch_shapes=[pltpu.VMEM(operand.shape, operand.dtype) for operand in operands] + [
            pltpu.VMEM((rows, LANES), jnp.float32),
            pltpu.VMEM((rows, LANES), jnp.float32),
            pltpu.VMEM((rows, LANES), jnp.int32),
            pltpu.VMEM((n, SUBLANES, width), jnp.float32),
            pltpu.VMEM((depth, plane, SUBLANES, width), jnp.float32),
            pltpu.VMEM((depth, SUBLANES, LANES), jnp.float32),
            pltpu.VMEM((depth, src_local, LANES), jnp.float32),
            pltpu.VMEM((depth, depth, 3 * SUBLANES, LANES), jnp.float32),
            pltpu.VMEM((n, SUBLANES, LANES), jnp.float32),
            pltpu.SemaphoreType.DMA((len(operands),)),
            pltpu.SemaphoreType.DMA,
            pltpu.SemaphoreType.DMA((depth, plane)),
            pltpu.SemaphoreType.DMA,
            pltpu.SemaphoreType.DMA,
            pltpu.SemaphoreType.DMA,
            pltpu.SemaphoreType.DMA((depth, depth)),
            pltpu.SemaphoreType.DMA,
            pltpu.SemaphoreType.DMA((depth,)),
        ],
        compiler_params=pltpu.CompilerParams(
            collective_id=0, has_side_effects=True, vmem_limit_bytes=65000 * 1024
        ),
        name="exchange_fit",
    )(*operands)
    results = (updates, standardized, norm)
    updates, standardized, norm = pl.pallas_call(
        release,
        out_shape=tuple(jax.ShapeDtypeStruct(r.shape, r.dtype) for r in results),
        in_specs=[vmem] * 3,
        out_specs=[pl.BlockSpec(memory_space=pltpu.HBM)] * 3,
        scratch_shapes=[pltpu.SemaphoreType.DMA((3,))],
        name="release",
    )(*results)
    standardized = standardized.reshape(n, width)[:, :block_rows] if width != block_rows else standardized
    return (updates, standardized.reshape(row_count), norm[0, 0])


def solution(mesh):
    in_specs = (
        P(("grp", "dev")),
        P(("grp", "dev")),
        P(),
        P(("grp", "dev")),
        P(None, ("grp", "dev")),
        P(("grp", "dev")),
        P(("grp", "dev")),
        P(None, ("grp", "dev")),
    )
    out_specs = (P(None, ("grp", "dev")), P(("grp", "dev")), P())
    return jax.shard_map(body, mesh=mesh, in_specs=in_specs, out_specs=out_specs, check_vma=False)
```

time: 30.9 us -> 29.1 us (0.942)
  Pallas kernels: 30 us -> 28.2 us
    pallas_call x1, Pallas kernels: 28.5 us -> 26.7 us  [body(): pl.pallas_call(functools.partial(kernel, (groups, members, width, row_cou...]
where the time goes in v1:
time: 29.1 us; the launch traced here: 28.8 us
  Pallas kernels  28.2 us (97%)
  between operations  0.64 us (2%)
    pallas_call x1, Pallas kernels, body(): pl.pallas_call(functools.partial(kernel, (groups, members, width, row_cou...  26.7 us
    pallas_call x1, Pallas kernels, body(): pl.pallas_call(release, out_shape=tuple((jax.ShapeDtypeStruct(r.shape, r....  1.5 us

profile of v1, /device:TPU:0, one launch (start us, length us, event | category | flops | bytes accessed | tf_op | source)
XLA Modules:
  0.0 28.8 jit_solution(13056006082873654186)
XLA Ops:
  0.6 26.7 %exchange_fit.1 = (f32[5,128]{1,0:T(8,128)}, f32[128,128]{1,0:T(8,128)}, f32[1,128]{1,0:T(1,128)}) custom-call(s32[128,128]{1,0:T(8,128)} %bitcast.9, s32[128,128]{1,0:T(8,128)} %bitcast.10, s32[32,128]{1,0:T(8,128)} %bitcast.13, s32[1,128]{1,0:T(1,128)} %bitcast.14, f32[5,16384]{1,0:T(8,128)} %partials_hbm.1, f32[128,128]{1,0:T(8,128)} %bitcast.11, ...), custom_call_target="tpu_custom_call" | custom-call | tf_op jit(solution)/shard_map/exchange_fit/pallas_call | solution.py:429
  27.3 1.5 %release.1 = (f32[5,128]{1,0:T(8,128)}, f32[128,128]{1,0:T(8,128)}, f32[1,128]{1,0:T(1,128)}) custom-call(f32[5,128]{1,0:T(8,128)} %get-tuple-element.9.a_ref, f32[128,128]{1,0:T(8,128)} %get-tuple-element.10.b_ref, f32[1,128]{1,0:T(1,128)} %get-tuple-element.11.c_ref), custom_call_target="tpu_custom_call" | custom-call | tf_op jit(solution)/shard_map/release/pallas_call | solution.py:464

commit v2 on v1

--- a/solution.py
+++ b/solution.py
@@ -58,7 +58,7 @@
     source_hbm, slot_hbm, owner_hbm, counts_hbm, partials_hbm, residual_hbm, weight_hbm, prior_hbm,
     updates_ref, fresh_ref, norm_ref,
     source_ref, slot_ref, owner_ref, counts_ref, partials_ref, residual_ref, weight_ref, prior_ref,
-    root_buf, cell_buf, place_buf, out_buf, in_buf, meta_buf, ends_buf, sums_buf, tables,
+    root_buf, cell_buf, place_buf, out_buf, in_buf, meta_buf, first_buf, ends_buf, sums_buf, tables,
     load_sem, send_sem, recv_sem, meta_send_sem, meta_recv_sem, sums_send_sem, sums_recv_sem,
     table_send_sem, table_recv_sem,
 ):
@@ -117,38 +117,10 @@
     for load in loads:
         load.wait()
 
-    meta_buf[my_depth] = jnp.concatenate(
-        [prior_ref[...], counts_ref[...].astype(jnp.float32), jnp.zeros((SUBLANES - items, LANES), jnp.float32)], axis=0
-    )
-    batch = min(32, owner_ref.shape[0])
-
-    def locate(step, carry):
-        rows = pl.ds(pl.multiple_of(step * SUBLANES, SUBLANES), SUBLANES)
-        source = source_ref[rows, :]
-        lane, tile = source % LANES, source // LANES
-
-        def look(group, found):
-            for t in range(batch):
-                row = group * batch + t
-                entry = jnp.broadcast_to(owner_ref[pl.ds(row, 1), :], (SUBLANES, LANES))
-                found = jnp.where(tile == row, gather_lanes(entry, lane), found)
-            return found
-
-        found = jnp.full((SUBLANES, LANES), -1, jnp.int32)
-        if owner_ref.shape[0] == batch:
-            found = look(0, found)
-        else:
-            found = lax.fori_loop(0, owner_ref.shape[0] // batch, look, found)
-        place = found % LANES
-        place_buf[rows, :] = place
-        cell = jnp.where(found < 0, -1, place * pad_slots + slot_ref[rows, :])
-        cell_buf[rows, :] = cell.astype(jnp.float32)
-        root = jnp.sqrt(weight_ref[rows, :])
-        root_buf[rows, :] = root
-        residual_ref[rows, :] = residual_ref[rows, :] * root
-        return carry
-
-    lax.fori_loop(0, source_ref.shape[0] // SUBLANES, locate, 0)
+    root = jnp.sqrt(weight_ref[...])
+    root_buf[...] = root
+    residual_ref[...] = residual_ref[...] * root
+    cell_buf[...] = (source_ref[...] * pad_slots + slot_ref[...]).astype(jnp.float32)
 
     sublane = lax.broadcasted_iota(jnp.int32, (SUBLANES, LANES), 0)
 
@@ -169,6 +141,25 @@
         return carry
 
     lax.fori_loop(0, n, prepare, 0)
+
+    src_local = counts_ref.shape[1]
+    square = (src_local, LANES)
+    row_index = lax.broadcasted_iota(jnp.int32, square, 0)
+    lane_index = lax.broadcasted_iota(jnp.int32, square, 1)
+    diagonal = row_index == lane_index
+
+    def invert(tile, total):
+        ids = tile * LANES + lax.broadcasted_iota(jnp.int32, (1, LANES), 1)
+        return total + jnp.where(owner_ref[pl.ds(tile, 1), :] == row_index + me * src_local, ids, 0)
+
+    found = lax.fori_loop(0, owner_ref.shape[0], invert, jnp.zeros(square, jnp.int32))
+    source_at = jnp.sum(found.astype(jnp.float32), axis=1, keepdims=True)
+    source_at = jnp.sum(jnp.where(diagonal, source_at, 0.0), axis=0, keepdims=True)
+    meta_buf[my_depth] = jnp.concatenate(
+        [prior_ref[...], counts_ref[...].astype(jnp.float32), source_at * pad_slots]
+        + [jnp.zeros((SUBLANES - words, LANES), jnp.float32)],
+        axis=0,
+    )
 
     pl.semaphore_wait(barrier, plane - 1 + depth - 1)
 
@@ -228,33 +219,30 @@
         device_id=level_coords((my_depth + 1) % depth), device_id_type=MESH,
     ).wait_recv()
 
-    src_local = counts_ref.shape[1]
-    square = (src_local, LANES)
-    first_cell = lax.broadcasted_iota(jnp.int32, square, 0) * pad_slots
-    diagonal = lax.broadcasted_iota(jnp.int32, square, 0) == lax.broadcasted_iota(jnp.int32, square, 1)
-    first_cell = first_cell.astype(jnp.float32)
-
-    def find_ends(level, carry):
-        counts = meta_buf[level, params:items, :]
-        column = jnp.sum(jnp.where(diagonal, counts, 0.0), axis=1, keepdims=True)
-        ends_buf[level] = first_cell + column
-        return carry
-
-    lax.fori_loop(0, depth, find_ends, 0)
+    def find_cells(level, carry):
+        first = jnp.sum(jnp.where(diagonal, meta_buf[level, items:words, :], 0.0), axis=1, keepdims=True)
+        counts = jnp.sum(jnp.where(diagonal, meta_buf[level, params:items, :], 0.0), axis=1, keepdims=True)
+        first_buf[level] = jnp.broadcast_to(first, square)
+        ends_buf[level] = jnp.broadcast_to(first + counts, square)
+        return carry
+
+    lax.fori_loop(0, depth, find_cells, 0)
     wide_sublane = lax.broadcasted_iota(jnp.int32, (SUBLANES, width), 0)
 
-    def absorb(level, slot):
-        rows = in_buf[level, slot]
-        cell = rows[items:words, :]
-        rows = jnp.where(wide_sublane < items, rows, 0.0)
-        end_cell = ends_buf[level]
-        hot = []
-        for piece in range(pieces):
-            part = cell[:, piece * LANES : (piece + 1) * LANES]
-            hit = jnp.logical_and(part >= first_cell, part < end_cell)
-            hot.append(jnp.where(hit, 1.0, 0.0))
+    def absorb(level, slots):
+        first_cell, end_cell = first_buf[level], ends_buf[level]
+        hot, products = [], []
+        for slot in slots:
+            rows = in_buf[level, slot]
+            cell = rows[items:words, :]
+            rows = jnp.where(wide_sublane < items, rows, 0.0)
+            for piece in range(pieces):
+                part = cell[:, piece * LANES : (piece + 1) * LANES]
+                hit = jnp.logical_and(part >= first_cell, part < end_cell)
+                hot.append(jnp.where(hit, 1.0, 0.0))
+            products.append(jnp.concatenate([rows[i : i + 1, :] * rows for i in range(items)], axis=0))
         hot = jnp.concatenate(hot, axis=1).astype(jnp.bfloat16)
-        products = jnp.concatenate([rows[i : i + 1, :] * rows for i in range(items)], axis=0)
+        products = jnp.concatenate(products, axis=1)
         return lax.dot_general(
             thirds(products), hot, (((1,), (1,)), ((), ())), preferred_element_type=jnp.float32
         )
@@ -262,16 +250,18 @@
     height = items * SUBLANES
 
     def gather_level(level, carry):
-        total = absorb(level, my_seat)
-
-        def arrive(step, total):
-            group, core = origin(plane - 1 - step)
-            seat = (group, core)
-            slot = group * CORES + core
-            row_copy(level, seat, slot).wait_recv()
-            return total + absorb(level, slot)
-
-        total = lax.fori_loop(0, plane - 1, arrive, total)
+        def arrive(steps):
+            slots = []
+            for step in steps:
+                group, core = origin(step)
+                slot = group * CORES + core
+                if step:
+                    row_copy(level, (group, core), slot).wait_recv()
+                slots.append(slot)
+            return absorb(level, slots)
+
+        half = plane // 2
+        total = arrive([0] + list(range(plane - 1, half, -1))) + arrive(range(half, 0, -1))
         total = total[0:height] + total[height : 2 * height] + total[2 * height : 3 * height]
         blocks = [total[i * SUBLANES : (i + 1) * SUBLANES] for i in range(items)]
         first = jnp.where(sublane == items, pltpu.roll(blocks[5], 1, 0), blocks[0])
@@ -289,6 +279,30 @@
         return carry
 
     lax.fori_loop(0, depth, gather_level, 0)
+    batch = min(32, owner_ref.shape[0])
+
+    def locate(step, carry):
+        rows = pl.ds(pl.multiple_of(step * SUBLANES, SUBLANES), SUBLANES)
+        source = source_ref[rows, :]
+        lane, tile = source % LANES, source // LANES
+
+        def look(group, found):
+            for t in range(batch):
+                row = group * batch + t
+                entry = jnp.broadcast_to(owner_ref[pl.ds(row, 1), :], (SUBLANES, LANES))
+                found = jnp.where(tile == row, gather_lanes(entry, lane), found)
+            return found
+
+        found = jnp.full((SUBLANES, LANES), -1, jnp.int32)
+        if owner_ref.shape[0] == batch:
+            found = look(0, found)
+        else:
+            found = lax.fori_loop(0, owner_ref.shape[0] // batch, look, found)
+        place_buf[rows, :] = found % LANES
+        return carry
+
+    lax.fori_loop(0, source_ref.shape[0] // SUBLANES, locate, 0)
+
 
     at = {(0, 0): 0, (0, 1): 1, (0, 2): 2, (0, 3): 3, (0, 4): 4, (0, 5): 5, (5, 5): 6,
           (3, 5): 8, (1, 1): 9, (1, 2): 10, (1, 3): 11, (1, 4): 12, (1, 5): 13, (3, 3): 14, (3, 4): 15,
@@ -337,7 +351,7 @@
     lax.fori_loop(0, depth, fit_level, 0)
     updates_ref[...] = tables[me, 0:params, :]
 
-    def refit_level(level, carry):
+    def refit_level(level, tails):
         seats = pl.ds(0, plane - 1)
         pltpu.make_async_remote_copy(
             src_ref=tables.at[seats], dst_ref=tables.at[seats],
@@ -345,9 +359,10 @@
             device_id=seat_coords(target(1)), device_id_type=MESH,
         ).wait_recv()
 
-        def refit(seat, carry):
+        for seat in range(plane):
             k = seat // CORES * members + level * CORES + seat % CORES
             table = tables[k]
+            tails = tails + table[items : words + 1, :]
             for piece in range(pieces):
                 row = pl.ds(k * pieces + piece, 1)
                 place = jnp.broadcast_to(place_buf[row, :], (SUBLANES, LANES))
@@ -356,16 +371,9 @@
                 fresh = -jnp.sum(jnp.where(sublane < items, picked * rows, 0.0), axis=0, keepdims=True)
                 live = rows[words : words + 1, :] < picked[words : words + 1, :]
                 root_buf[row, :] = jnp.where(live, fresh, 0.0)
-            return carry
-
-        return lax.fori_loop(0, plane, refit, carry)
-
-    lax.fori_loop(0, depth, refit_level, 0)
-
-    def tally(k, tails):
-        return tails + tables[k, items : words + 1, :]
-
-    tails = lax.fori_loop(0, n, tally, jnp.zeros((2, LANES), jnp.float32))
+        return tails
+
+    tails = lax.fori_loop(0, depth, refit_level, jnp.zeros((2, LANES), jnp.float32))
     tails = jnp.sum(tails, axis=1, keepdims=True)
     norm = jnp.sqrt(jnp.maximum(tails[0:1], 0.0) / tails[1:2] + 1e-06)
     norm_ref[...] = jnp.broadcast_to(norm, norm_ref.shape)
@@ -425,13 +433,14 @@
         dense(weight, 1),
         prior,
     )
+    operands = tuple(pltpu.with_memory_space_constraint(x, pltpu.HBM) for x in operands)
     rows = n * width // LANES
     updates, standardized, norm = pl.pallas_call(
         functools.partial(kernel, (groups, members, width, row_count // src_local)),
         out_shape=(
-            jax.ShapeDtypeStruct((params, src_local), jnp.float32),
-            jax.ShapeDtypeStruct((rows, LANES), jnp.float32),
-            jax.ShapeDtypeStruct((1, LANES), jnp.float32),
+            pltpu.VMEM((params, src_local), jnp.float32),
+            pltpu.VMEM((rows, LANES), jnp.float32),
+            pltpu.VMEM((1, LANES), jnp.float32),
         ),
         in_specs=[pl.BlockSpec(memory_space=pltpu.HBM)] * len(operands),
         out_specs=(vmem, vmem, vmem),
@@ -442,6 +451,7 @@
             pltpu.VMEM((n, SUBLANES, width), jnp.float32),
             pltpu.VMEM((depth, plane, SUBLANES, width), jnp.float32),
             pltpu.VMEM((depth, SUBLANES, LANES), jnp.float32),
+            pltpu.VMEM((depth, src_local, LANES), jnp.float32),
             pltpu.VMEM((depth, src_local, LANES), jnp.float32),
             pltpu.VMEM((depth, depth, 3 * SUBLANES, LANES), jnp.float32),
             pltpu.VMEM((n, SUBLANES, LANES), jnp.float32),
@@ -456,7 +466,7 @@
             pltpu.SemaphoreType.DMA((depth,)),
         ],
         compiler_params=pltpu.CompilerParams(
-            collective_id=0, has_side_effects=True, vmem_limit_bytes=65000 * 1024
+            collective_id=0, has_side_effects=True, vmem_limit_bytes=40 << 20
         ),
         name="exchange_fit",
     )(*operands)
@@ -467,6 +477,7 @@
         in_specs=[vmem] * 3,
         out_specs=[pl.BlockSpec(memory_space=pltpu.HBM)] * 3,
         scratch_shapes=[pltpu.SemaphoreType.DMA((3,))],
+        compiler_params=pltpu.CompilerParams(vmem_limit_bytes=4 << 20),
         name="release",
     )(*results)
     standardized = standardized.reshape(n, width)[:, :block_rows] if width != block_rows else standardized

time: 29.1 us -> 23 us (0.79)
  Pallas kernels: 28.2 us -> 22.1 us
    pallas_call x1, Pallas kernels: 26.7 us -> 21.4 us  [body(): pl.pallas_call(functools.partial(kernel, (groups, members, width, row_cou...]
    pallas_call x1, Pallas kernels: 1.5 us -> 0.66 us  [body(): pl.pallas_call(release, out_shape=tuple((jax.ShapeDtypeStruct(r.shape, r....]
where the time goes in v2:
time: 23 us; the launch traced here: 22.7 us
  Pallas kernels  22.1 us (96%)
  between operations  0.64 us (3%)
    pallas_call x1, Pallas kernels, body(): pl.pallas_call(functools.partial(kernel, (groups, members, width, row_cou...  21.4 us
    pallas_call x1, Pallas kernels, body(): pl.pallas_call(release, out_shape=tuple((jax.ShapeDtypeStruct(r.shape, r....  0.66 us

profile of v2, /device:TPU:0, one launch (start us, length us, event | category | flops | bytes accessed | tf_op | source)
XLA Modules:
  0.0 22.7 jit_solution(16476760805539168458)
XLA Ops:
  0.6 21.4 %exchange_fit.1 = (f32[5,128]{1,0:T(8,128)S(1)}, f32[128,128]{1,0:T(8,128)S(1)}, f32[1,128]{1,0:T(1,128)S(1)}) custom-call(s32[128,128]{1,0:T(8,128)} %bitcast.9, s32[128,128]{1,0:T(8,128)} %bitcast.10, s32[32,128]{1,0:T(8,128)} %bitcast.13, s32[1,128]{1,0:T(1,128)} %bitcast.14, f32[5,16384]{1,0:T(8,128)} %partials_hbm.1, f32[128,128]{1,0:T(8,128)} %bitcast.11, ...), custom_call_target="tpu_custom_call" | custom-call | tf_op jit(solution)/shard_map/exchange_fit/pallas_call | solution.py:438
  22.1 0.7 %release.1 = (f32[5,128]{1,0:T(8,128)}, f32[128,128]{1,0:T(8,128)}, f32[1,128]{1,0:T(1,128)}) custom-call(f32[5,128]{1,0:T(8,128)S(1)} %get-tuple-element.9.a_ref, f32[128,128]{1,0:T(8,128)S(1)} %get-tuple-element.10.b_ref, f32[1,128]{1,0:T(1,128)S(1)} %get-tuple-element.11.c_ref), custom_call_target="tpu_custom_call" | custom-call | tf_op jit(solution)/shard_map/release/pallas_call | solution.py:474

commit v3 on v2

--- a/solution.py
+++ b/solution.py
@@ -43,10 +43,11 @@
 
 
 def thirds(values):
-    high = values.astype(jnp.bfloat16).astype(jnp.float32)
-    rest = values - high
-    middle = rest.astype(jnp.bfloat16).astype(jnp.float32)
-    return jnp.concatenate([high, middle, rest - middle], axis=0).astype(jnp.bfloat16)
+    high = values.astype(jnp.bfloat16)
+    rest = values - high.astype(jnp.float32)
+    middle = rest.astype(jnp.bfloat16)
+    last = (rest - middle.astype(jnp.float32)).astype(jnp.bfloat16)
+    return jnp.concatenate([high, middle, last], axis=0)
 
 
 def gather_lanes(table, index):
@@ -58,7 +59,7 @@
     source_hbm, slot_hbm, owner_hbm, counts_hbm, partials_hbm, residual_hbm, weight_hbm, prior_hbm,
     updates_ref, fresh_ref, norm_ref,
     source_ref, slot_ref, owner_ref, counts_ref, partials_ref, residual_ref, weight_ref, prior_ref,
-    root_buf, cell_buf, place_buf, out_buf, in_buf, meta_buf, first_buf, ends_buf, sums_buf, tables,
+    root_buf, cell_buf, place_buf, out_buf, in_buf, meta_buf, first_buf, room_buf, sums_buf, tables,
     load_sem, send_sem, recv_sem, meta_send_sem, meta_recv_sem, sums_send_sem, sums_recv_sem,
     table_send_sem, table_recv_sem,
 ):
@@ -72,6 +73,40 @@
     pieces = width // LANES
     low = 2 if groups % 2 == 0 else 1
     high = groups // low
+    my_group, my_member = lax.axis_index("grp"), lax.axis_index("dev")
+    my_depth, my_core = my_member // CORES, my_member % CORES
+    me = my_group * members + my_member
+    my_seat = my_group * CORES + my_core
+
+    def target(step):
+        jump = step // CORES
+        group = (my_group // low + jump // low) % high * low + (my_group % low + jump % low) % low
+        return group, (my_core + step % CORES) % CORES
+
+    def origin(step):
+        jump = step // CORES
+        group = (my_group // low + high - jump // low) % high * low + (my_group % low + low - jump % low) % low
+        return group, (my_core + CORES - step % CORES) % CORES
+
+    def seat_coords(seat):
+        group, core = seat
+        return (group, my_depth * CORES + core)
+
+    def level_coords(level):
+        return (my_group, level * CORES + my_core)
+
+    barrier = pltpu.get_barrier_semaphore()
+
+    def greet(step, carry):
+        pl.semaphore_signal(barrier, inc=1, device_id=seat_coords(target(step)), device_id_type=MESH)
+        return carry
+
+    def greet_level(step, carry):
+        pl.semaphore_signal(barrier, inc=1, device_id=level_coords((my_depth + step) % depth), device_id_type=MESH)
+        return carry
+
+    lax.fori_loop(1, depth, greet_level, 0)
+    lax.fori_loop(1, plane, greet, 0)
     row_pairs = (
         (owner_hbm, owner_ref), (source_hbm, source_ref), (slot_hbm, slot_ref), (weight_hbm, weight_ref),
         (residual_hbm, residual_ref), (partials_hbm, partials_ref), (counts_hbm, counts_ref), (prior_hbm, prior_ref),
@@ -79,40 +114,6 @@
     loads = [pltpu.make_async_copy(a, b, load_sem.at[i]) for i, (a, b) in enumerate(row_pairs)]
     for load in loads:
         load.start()
-    my_group, my_member = lax.axis_index("grp"), lax.axis_index("dev")
-    my_depth, my_core = my_member // CORES, my_member % CORES
-    me = my_group * members + my_member
-    my_seat = my_group * CORES + my_core
-
-    def target(step):
-        jump = step // CORES
-        group = (my_group // low + jump // low) % high * low + (my_group % low + jump % low) % low
-        return group, (my_core + step % CORES) % CORES
-
-    def origin(step):
-        jump = step // CORES
-        group = (my_group // low + high - jump // low) % high * low + (my_group % low + low - jump % low) % low
-        return group, (my_core + CORES - step % CORES) % CORES
-
-    def seat_coords(seat):
-        group, core = seat
-        return (group, my_depth * CORES + core)
-
-    def level_coords(level):
-        return (my_group, level * CORES + my_core)
-
-    barrier = pltpu.get_barrier_semaphore()
-
-    def greet(step, carry):
-        pl.semaphore_signal(barrier, inc=1, device_id=seat_coords(target(step)), device_id_type=MESH)
-        return carry
-
-    def greet_level(step, carry):
-        pl.semaphore_signal(barrier, inc=1, device_id=level_coords((my_depth + step) % depth), device_id_type=MESH)
-        return carry
-
-    lax.fori_loop(1, depth, greet_level, 0)
-    lax.fori_loop(1, plane, greet, 0)
 
     for load in loads:
         load.wait()
@@ -142,17 +143,71 @@
 
     lax.fori_loop(0, n, prepare, 0)
 
+    pl.semaphore_wait(barrier, plane - 1 + depth - 1)
+
+    def meta_copy(level, slot):
+        return pltpu.make_async_remote_copy(
+            src_ref=meta_buf.at[slot], dst_ref=meta_buf.at[slot], send_sem=meta_send_sem, recv_sem=meta_recv_sem,
+            device_id=level_coords(level), device_id_type=MESH,
+        )
+
+    def row_copy(level, seat, slot, part):
+        group, core = seat
+        return pltpu.make_async_remote_copy(
+            src_ref=out_buf.at[group * members + level * CORES + core, pl.ds(0, words)],
+            dst_ref=in_buf.at[level, slot, pl.ds(0, words)],
+            send_sem=send_sem, recv_sem=recv_sem.at[level, part],
+            device_id=seat_coords(seat), device_id_type=MESH,
+        )
+
+    def sums_copy(level, stage, slot):
+        return pltpu.make_async_remote_copy(
+            src_ref=sums_buf.at[slot, stage], dst_ref=sums_buf.at[slot, stage],
+            send_sem=sums_send_sem, recv_sem=sums_recv_sem.at[stage],
+            device_id=level_coords(level), device_id_type=MESH,
+        )
+
+    def table_copy(stage, seat, slot):
+        return pltpu.make_async_remote_copy(
+            src_ref=tables.at[slot], dst_ref=tables.at[slot],
+            send_sem=table_send_sem, recv_sem=table_recv_sem.at[stage],
+            device_id=seat_coords(seat), device_id_type=MESH,
+        )
+
+    half = plane // 2
+    batches = ([0] + list(range(plane - 1, half, -1)), list(range(half, 0, -1)))
+
+    def send_rows(level, carry):
+        for part, steps in enumerate(batches):
+            for step in steps:
+                if step:
+                    row_copy(level, target(step), my_seat, part).start()
+        return carry
+
+    lax.fori_loop(0, depth, send_rows, 0)
+
+    def own_rows(level, carry):
+        in_buf[level, my_seat] = out_buf[my_group * members + level * CORES + my_core]
+        return carry
+
+    lax.fori_loop(0, depth, own_rows, 0)
+
     src_local = counts_ref.shape[1]
     square = (src_local, LANES)
     row_index = lax.broadcasted_iota(jnp.int32, square, 0)
     lane_index = lax.broadcasted_iota(jnp.int32, square, 1)
     diagonal = row_index == lane_index
 
-    def invert(tile, total):
-        ids = tile * LANES + lax.broadcasted_iota(jnp.int32, (1, LANES), 1)
-        return total + jnp.where(owner_ref[pl.ds(tile, 1), :] == row_index + me * src_local, ids, 0)
-
-    found = lax.fori_loop(0, owner_ref.shape[0], invert, jnp.zeros(square, jnp.int32))
+    spare = 4
+
+    def invert(step, total):
+        for part in range(spare):
+            tile = step * spare + part
+            ids = tile * LANES + lane_index
+            total = jnp.where(owner_ref[pl.ds(tile, 1), :] == row_index + me * src_local, ids, total)
+        return total
+
+    found = lax.fori_loop(0, owner_ref.shape[0] // spare, invert, jnp.zeros(square, jnp.int32))
     source_at = jnp.sum(found.astype(jnp.float32), axis=1, keepdims=True)
     source_at = jnp.sum(jnp.where(diagonal, source_at, 0.0), axis=0, keepdims=True)
     meta_buf[my_depth] = jnp.concatenate(
@@ -161,124 +216,12 @@
         axis=0,
     )
 
-    pl.semaphore_wait(barrier, plane - 1 + depth - 1)
-
-    def meta_copy(level, slot):
-        return pltpu.make_async_remote_copy(
-            src_ref=meta_buf.at[slot], dst_ref=meta_buf.at[slot], send_sem=meta_send_sem, recv_sem=meta_recv_sem,
-            device_id=level_coords(level), device_id_type=MESH,
-        )
-
-    def row_copy(level, seat, slot):
-        group, core = seat
-        return pltpu.make_async_remote_copy(
-            src_ref=out_buf.at[group * members + level * CORES + core, pl.ds(0, words)],
-            dst_ref=in_buf.at[level, slot, pl.ds(0, words)],
-            send_sem=send_sem, recv_sem=recv_sem.at[level, slot],
-            device_id=seat_coords(seat), device_id_type=MESH,
-        )
-
-    def sums_copy(level, stage, slot):
-        return pltpu.make_async_remote_copy(
-            src_ref=sums_buf.at[slot, stage], dst_ref=sums_buf.at[slot, stage],
-            send_sem=sums_send_sem, recv_sem=sums_recv_sem.at[stage, slot],
-            device_id=level_coords(level), device_id_type=MESH,
-        )
-
-    def table_copy(stage, seat, slot):
-        return pltpu.make_async_remote_copy(
-            src_ref=tables.at[slot], dst_ref=tables.at[slot],
-            send_sem=table_send_sem, recv_sem=table_recv_sem.at[stage],
-            device_id=seat_coords(seat), device_id_type=MESH,
-        )
-
     def send_meta(step, carry):
         meta_copy((my_depth + step) % depth, my_depth).start()
         return carry
 
     lax.fori_loop(1, depth, send_meta, 0)
 
-    def send_rows(level, carry):
-        def send_one(step, carry):
-            row_copy(level, target(plane - 1 - step), my_seat).start()
-            return carry
-
-        return lax.fori_loop(0, plane - 1, send_one, carry)
-
-    lax.fori_loop(0, depth, send_rows, 0)
-
-    def own_rows(level, carry):
-        in_buf[level, my_seat] = out_buf[my_group * members + level * CORES + my_core]
-        return carry
-
-    lax.fori_loop(0, depth, own_rows, 0)
-
-    others = pl.ds(0, depth - 1)
-    pltpu.make_async_remote_copy(
-        src_ref=meta_buf.at[others], dst_ref=meta_buf.at[others], send_sem=meta_send_sem, recv_sem=meta_recv_sem,
-        device_id=level_coords((my_depth + 1) % depth), device_id_type=MESH,
-    ).wait_recv()
-
-    def find_cells(level, carry):
-        first = jnp.sum(jnp.where(diagonal, meta_buf[level, items:words, :], 0.0), axis=1, keepdims=True)
-        counts = jnp.sum(jnp.where(diagonal, meta_buf[level, params:items, :], 0.0), axis=1, keepdims=True)
-        first_buf[level] = jnp.broadcast_to(first, square)
-        ends_buf[level] = jnp.broadcast_to(first + counts, square)
-        return carry
-
-    lax.fori_loop(0, depth, find_cells, 0)
-    wide_sublane = lax.broadcasted_iota(jnp.int32, (SUBLANES, width), 0)
-
-    def absorb(level, slots):
-        first_cell, end_cell = first_buf[level], ends_buf[level]
-        hot, products = [], []
-        for slot in slots:
-            rows = in_buf[level, slot]
-            cell = rows[items:words, :]
-            rows = jnp.where(wide_sublane < items, rows, 0.0)
-            for piece in range(pieces):
-                part = cell[:, piece * LANES : (piece + 1) * LANES]
-                hit = jnp.logical_and(part >= first_cell, part < end_cell)
-                hot.append(jnp.where(hit, 1.0, 0.0))
-            products.append(jnp.concatenate([rows[i : i + 1, :] * rows for i in range(items)], axis=0))
-        hot = jnp.concatenate(hot, axis=1).astype(jnp.bfloat16)
-        products = jnp.concatenate(products, axis=1)
-        return lax.dot_general(
-            thirds(products), hot, (((1,), (1,)), ((), ())), preferred_element_type=jnp.float32
-        )
-
-    height = items * SUBLANES
-
-    def gather_level(level, carry):
-        def arrive(steps):
-            slots = []
-            for step in steps:
-                group, core = origin(step)
-                slot = group * CORES + core
-                if step:
-                    row_copy(level, (group, core), slot).wait_recv()
-                slots.append(slot)
-            return absorb(level, slots)
-
-        half = plane // 2
-        total = arrive([0] + list(range(plane - 1, half, -1))) + arrive(range(half, 0, -1))
-        total = total[0:height] + total[height : 2 * height] + total[2 * height : 3 * height]
-        blocks = [total[i * SUBLANES : (i + 1) * SUBLANES] for i in range(items)]
-        first = jnp.where(sublane == items, pltpu.roll(blocks[5], 1, 0), blocks[0])
-        second = jnp.where(
-            jnp.logical_or(sublane == 0, sublane >= items), pltpu.roll(blocks[3], 3, 0), blocks[1]
-        )
-        third = jnp.where(sublane < 2, pltpu.roll(blocks[4], 4, 0), blocks[2])
-        sums_buf[my_depth, level] = jnp.concatenate([first, second, third], axis=0)
-
-        def send_sums(step, carry):
-            sums_copy((my_depth + step) % depth, level, my_depth).start()
-            return carry
-
-        lax.fori_loop(1, depth, send_sums, 0)
-        return carry
-
-    lax.fori_loop(0, depth, gather_level, 0)
     batch = min(32, owner_ref.shape[0])
 
     def locate(step, carry):
@@ -304,17 +247,93 @@
     lax.fori_loop(0, source_ref.shape[0] // SUBLANES, locate, 0)
 
 
+    others = pl.ds(0, depth - 1)
+    pltpu.make_async_remote_copy(
+        src_ref=meta_buf.at[others], dst_ref=meta_buf.at[others], send_sem=meta_send_sem, recv_sem=meta_recv_sem,
+        device_id=level_coords((my_depth + 1) % depth), device_id_type=MESH,
+    ).wait_recv()
+
+    def find_cells(level, carry):
+        first, counts = meta_buf[level, items:words, :], meta_buf[level, params:items, :]
+        first = jnp.sum(jnp.where(diagonal, first, 0.0), axis=1, keepdims=True)
+        counts = jnp.sum(jnp.where(diagonal, counts, 0.0), axis=1, keepdims=True)
+        first_buf[level] = jnp.broadcast_to(first, square).astype(jnp.int32)
+        room_buf[level] = jnp.broadcast_to(counts, square).astype(jnp.int32).astype(jnp.uint32)
+        return carry
+
+    lax.fori_loop(0, depth, find_cells, 0, unroll=depth if depth <= 4 else 1)
+    wide_sublane = lax.broadcasted_iota(jnp.int32, (SUBLANES, width), 0)
+
+    low_rows = wide_sublane < 2
+    sixth_row = wide_sublane == items
+    outer_rows = jnp.logical_or(wide_sublane == 0, wide_sublane >= items)
+
+    def absorb(level, slot, sign):
+        first_cell, room = first_buf[level], room_buf[level]
+        rows = in_buf[level, slot]
+
+        def spread(i):
+            return jnp.broadcast_to(in_buf[level, slot, i : i + 1, :], (SUBLANES, width))
+
+        hot = []
+        for piece in range(pieces):
+            part = in_buf[level, slot, items:words, piece * LANES : (piece + 1) * LANES].astype(jnp.int32)
+            hit = (part - first_cell).astype(jnp.uint32) < room
+            hot.append(jnp.where(hit, sign, 0.0))
+        hot = jnp.concatenate(hot, axis=1).astype(jnp.bfloat16)
+        products = jnp.concatenate(
+            [
+                jnp.where(sixth_row, spread(5), spread(0)) * jnp.where(sixth_row, pltpu.roll(rows, 1, 0), rows),
+                jnp.where(outer_rows, spread(3), spread(1)) * jnp.where(outer_rows, pltpu.roll(rows, 3, 0), rows),
+                jnp.where(low_rows, spread(4), spread(2)) * jnp.where(low_rows, pltpu.roll(rows, 4, 0), rows),
+                jnp.zeros((SUBLANES, width), jnp.float32),
+            ],
+            axis=0,
+        )
+        return lax.dot_general(
+            thirds(products), hot, (((1,), (1,)), ((), ())), preferred_element_type=jnp.float32
+        )
+
+    height = 4 * SUBLANES
+
+    def gather_level(level, carry):
+        totals = [None, None]
+        for part, steps in enumerate(batches):
+            def batch_rows(count):
+                return in_buf.at[level, pl.ds(0, count), pl.ds(0, words)]
+
+            count = len([step for step in steps if step])
+            pltpu.make_async_remote_copy(
+                src_ref=batch_rows(count), dst_ref=batch_rows(count), send_sem=send_sem,
+                recv_sem=recv_sem.at[level, part], device_id=seat_coords(target(1)), device_id_type=MESH,
+            ).wait_recv()
+            for spot, step in enumerate(steps):
+                group, core = origin(step)
+                lane = spot % 2
+                part_sum = absorb(level, group * CORES + core, 1.0 - 2.0 * lane)
+                totals[lane] = part_sum if totals[lane] is None else totals[lane] + part_sum
+        total = totals[0] - totals[1]
+        total = total[0:height] + total[height : 2 * height] + total[2 * height : 3 * height]
+        sums_buf[my_depth, level] = total[0 : 3 * SUBLANES]
+
+        def send_sums(step, carry):
+            sums_copy((my_depth + step) % depth, level, my_depth).start()
+            return carry
+
+        lax.fori_loop(1, depth, send_sums, 0)
+        return carry
+
+    lax.fori_loop(0, depth, gather_level, 0)
     at = {(0, 0): 0, (0, 1): 1, (0, 2): 2, (0, 3): 3, (0, 4): 4, (0, 5): 5, (5, 5): 6,
           (3, 5): 8, (1, 1): 9, (1, 2): 10, (1, 3): 11, (1, 4): 12, (1, 5): 13, (3, 3): 14, (3, 4): 15,
           (4, 4): 16, (4, 5): 17, (2, 2): 18, (2, 3): 19, (2, 4): 20, (2, 5): 21}
 
     def fit_level(level, carry):
-        def fetch(step, carry):
-            other = (my_depth + depth - step) % depth
-            sums_copy(other, level, other).wait_recv()
-            return carry
-
-        lax.fori_loop(1, depth, fetch, 0)
+        pltpu.make_async_remote_copy(
+            src_ref=sums_buf.at[others, level], dst_ref=sums_buf.at[others, level],
+            send_sem=sums_send_sem, recv_sem=sums_recv_sem.at[level],
+            device_id=level_coords((my_depth + 1) % depth), device_id_type=MESH,
+        ).wait_recv()
 
         def gather_sums(slot, total):
             return total + sums_buf[slot, level]
@@ -451,17 +470,17 @@
             pltpu.VMEM((n, SUBLANES, width), jnp.float32),
             pltpu.VMEM((depth, plane, SUBLANES, width), jnp.float32),
             pltpu.VMEM((depth, SUBLANES, LANES), jnp.float32),
-            pltpu.VMEM((depth, src_local, LANES), jnp.float32),
-            pltpu.VMEM((depth, src_local, LANES), jnp.float32),
+            pltpu.VMEM((depth, src_local, LANES), jnp.int32),
+            pltpu.VMEM((depth, src_local, LANES), jnp.uint32),
             pltpu.VMEM((depth, depth, 3 * SUBLANES, LANES), jnp.float32),
             pltpu.VMEM((n, SUBLANES, LANES), jnp.float32),
             pltpu.SemaphoreType.DMA((len(operands),)),
             pltpu.SemaphoreType.DMA,
-            pltpu.SemaphoreType.DMA((depth, plane)),
+            pltpu.SemaphoreType.DMA((depth, 2)),
             pltpu.SemaphoreType.DMA,
             pltpu.SemaphoreType.DMA,
             pltpu.SemaphoreType.DMA,
-            pltpu.SemaphoreType.DMA((depth, depth)),
+            pltpu.SemaphoreType.DMA((depth,)),
             pltpu.SemaphoreType.DMA,
             pltpu.SemaphoreType.DMA((depth,)),
         ],

time: 23 us -> 22.5 us (0.978)
  Pallas kernels: 22.1 us -> 21.6 us
    pallas_call x1, Pallas kernels: 21.4 us -> 21 us  [body(): pl.pallas_call(functools.partial(kernel, (groups, members, width, row_cou...]
where the time goes in v3:
time: 22.5 us; the launch traced here: 22.3 us
  Pallas kernels  21.6 us (96%)
  between operations  0.64 us (3%)
    pallas_call x1, Pallas kernels, body(): pl.pallas_call(functools.partial(kernel, (groups, members, width, row_cou...  21 us
    pallas_call x1, Pallas kernels, body(): pl.pallas_call(release, out_shape=tuple((jax.ShapeDtypeStruct(r.shape, r....  0.66 us

profile of v3, /device:TPU:0, one launch (start us, length us, event | category | flops | bytes accessed | tf_op | source)
XLA Modules:
  0.0 22.3 jit_solution(8250429536587164180)
XLA Ops:
  0.6 21.0 %exchange_fit.1 = (f32[5,128]{1,0:T(8,128)S(1)}, f32[128,128]{1,0:T(8,128)S(1)}, f32[1,128]{1,0:T(1,128)S(1)}) custom-call(s32[128,128]{1,0:T(8,128)} %bitcast.9, s32[128,128]{1,0:T(8,128)} %bitcast.10, s32[32,128]{1,0:T(8,128)} %bitcast.13, s32[1,128]{1,0:T(1,128)} %bitcast.14, f32[5,16384]{1,0:T(8,128)} %partials_hbm.1, f32[128,128]{1,0:T(8,128)} %bitcast.11, ...), custom_call_target="tpu_custom_call" | custom-call | tf_op jit(solution)/shard_map/exchange_fit/pallas_call | solution.py:457
  21.6 0.7 %release.1 = (f32[5,128]{1,0:T(8,128)}, f32[128,128]{1,0:T(8,128)}, f32[1,128]{1,0:T(1,128)}) custom-call(f32[5,128]{1,0:T(8,128)S(1)} %get-tuple-element.9.a_ref, f32[128,128]{1,0:T(8,128)S(1)} %get-tuple-element.10.b_ref, f32[1,128]{1,0:T(1,128)S(1)} %get-tuple-element.11.c_ref), custom_call_target="tpu_custom_call" | custom-call | tf_op jit(solution)/shard_map/release/pallas_call | solution.py:493

commit v4 on v3

--- a/solution.py
+++ b/solution.py
@@ -73,40 +73,6 @@
     pieces = width // LANES
     low = 2 if groups % 2 == 0 else 1
     high = groups // low
-    my_group, my_member = lax.axis_index("grp"), lax.axis_index("dev")
-    my_depth, my_core = my_member // CORES, my_member % CORES
-    me = my_group * members + my_member
-    my_seat = my_group * CORES + my_core
-
-    def target(step):
-        jump = step // CORES
-        group = (my_group // low + jump // low) % high * low + (my_group % low + jump % low) % low
-        return group, (my_core + step % CORES) % CORES
-
-    def origin(step):
-        jump = step // CORES
-        group = (my_group // low + high - jump // low) % high * low + (my_group % low + low - jump % low) % low
-        return group, (my_core + CORES - step % CORES) % CORES
-
-    def seat_coords(seat):
-        group, core = seat
-        return (group, my_depth * CORES + core)
-
-    def level_coords(level):
-        return (my_group, level * CORES + my_core)
-
-    barrier = pltpu.get_barrier_semaphore()
-
-    def greet(step, carry):
-        pl.semaphore_signal(barrier, inc=1, device_id=seat_coords(target(step)), device_id_type=MESH)
-        return carry
-
-    def greet_level(step, carry):
-        pl.semaphore_signal(barrier, inc=1, device_id=level_coords((my_depth + step) % depth), device_id_type=MESH)
-        return carry
-
-    lax.fori_loop(1, depth, greet_level, 0)
-    lax.fori_loop(1, plane, greet, 0)
     row_pairs = (
         (owner_hbm, owner_ref), (source_hbm, source_ref), (slot_hbm, slot_ref), (weight_hbm, weight_ref),
         (residual_hbm, residual_ref), (partials_hbm, partials_ref), (counts_hbm, counts_ref), (prior_hbm, prior_ref),
@@ -114,6 +80,39 @@
     loads = [pltpu.make_async_copy(a, b, load_sem.at[i]) for i, (a, b) in enumerate(row_pairs)]
     for load in loads:
         load.start()
+    my_group, my_member = lax.axis_index("grp"), lax.axis_index("dev")
+    my_depth, my_core = my_member // CORES, my_member % CORES
+    me = my_group * members + my_member
+    my_seat = my_group * CORES + my_core
+
+    def target(step):
+        jump = step // CORES
+        group = (my_group // low + jump // low) % high * low + (my_group % low + jump % low) % low
+        return group, (my_core + step % CORES) % CORES
+
+    def origin(step):
+        jump = step // CORES
+        group = (my_group // low + high - jump // low) % high * low + (my_group % low + low - jump % low) % low
+        return group, (my_core + CORES - step % CORES) % CORES
+
+    def seat_coords(seat):
+        group, core = seat
+        return (group, my_depth * CORES + core)
+
+    def level_coords(level):
+        return (my_group, level * CORES + my_core)
+
+    barrier = pltpu.get_barrier_semaphore()
+    few = depth <= 4
+    used = 3 * SUBLANES - 2
+
+    def greet_level(step, carry):
+        pl.semaphore_signal(barrier, inc=1, device_id=level_coords((my_depth + step) % depth), device_id_type=MESH)
+        return carry
+
+    lax.fori_loop(1, depth, greet_level, 0, unroll=few)
+    for step in range(plane - 1, 0, -1):
+        pl.semaphore_signal(barrier, inc=1, device_id=seat_coords(target(step)), device_id_type=MESH)
 
     for load in loads:
         load.wait()
@@ -125,7 +124,8 @@
 
     sublane = lax.broadcasted_iota(jnp.int32, (SUBLANES, LANES), 0)
 
-    def prepare(k, carry):
+    def prepare(level, seat, carry):
+        k = seat // CORES * members + level * CORES + seat % CORES
         for piece in range(pieces):
             row = pl.ds(k * pieces + piece, 1)
             cols = pl.ds(pl.multiple_of(k * width + piece * LANES, LANES), LANES)
@@ -141,7 +141,10 @@
             out_buf[k, words : words + 1, part] = slot_ref[row, :].astype(jnp.float32)
         return carry
 
-    lax.fori_loop(0, n, prepare, 0)
+    def prepare_level(level, carry):
+        return lax.fori_loop(0, plane, functools.partial(prepare, level), carry, unroll=2)
+
+    prepare_level(0, 0)
 
     pl.semaphore_wait(barrier, plane - 1 + depth - 1)
 
@@ -162,7 +165,7 @@
 
     def sums_copy(level, stage, slot):
         return pltpu.make_async_remote_copy(
-            src_ref=sums_buf.at[slot, stage], dst_ref=sums_buf.at[slot, stage],
+            src_ref=sums_buf.at[slot, stage, pl.ds(0, used)], dst_ref=sums_buf.at[slot, stage, pl.ds(0, used)],
             send_sem=sums_send_sem, recv_sem=sums_recv_sem.at[stage],
             device_id=level_coords(level), device_id_type=MESH,
         )
@@ -177,14 +180,19 @@
     half = plane // 2
     batches = ([0] + list(range(plane - 1, half, -1)), list(range(half, 0, -1)))
 
-    def send_rows(level, carry):
+    def send_rows(level):
         for part, steps in enumerate(batches):
             for step in steps:
                 if step:
                     row_copy(level, target(step), my_seat, part).start()
-        return carry
-
-    lax.fori_loop(0, depth, send_rows, 0)
+
+    def stream_rows(level, carry):
+        prepare_level(level, 0)
+        send_rows(level - 1)
+        return carry
+
+    lax.fori_loop(1, depth, stream_rows, 0)
+    send_rows(depth - 1)
 
     def own_rows(level, carry):
         in_buf[level, my_seat] = out_buf[my_group * members + level * CORES + my_core]
@@ -320,7 +328,7 @@
             sums_copy((my_depth + step) % depth, level, my_depth).start()
             return carry
 
-        lax.fori_loop(1, depth, send_sums, 0)
+        lax.fori_loop(1, depth, send_sums, 0, unroll=few)
         return carry
 
     lax.fori_loop(0, depth, gather_level, 0)
@@ -330,15 +338,15 @@
 
     def fit_level(level, carry):
         pltpu.make_async_remote_copy(
-            src_ref=sums_buf.at[others, level], dst_ref=sums_buf.at[others, level],
+            src_ref=sums_buf.at[others, level, pl.ds(0, used)], dst_ref=sums_buf.at[others, level, pl.ds(0, used)],
             send_sem=sums_send_sem, recv_sem=sums_recv_sem.at[level],
             device_id=level_coords((my_depth + 1) % depth), device_id_type=MESH,
         ).wait_recv()
 
         def gather_sums(slot, total):
-            return total + sums_buf[slot, level]
-
-        total = lax.fori_loop(1, depth, gather_sums, sums_buf[0, level])
+            return total + sums_buf[slot, level, 0:used, :]
+
+        total = lax.fori_loop(1, depth, gather_sums, sums_buf[0, level, 0:used, :], unroll=few)
 
         def entry(i, j):
             spot = at[min(i, j), max(i, j)]
@@ -360,15 +368,18 @@
         mine = my_group * members + level * CORES + my_core
         tables[mine] = jnp.concatenate(updates + [jnp.full((1, LANES), -1.0, jnp.float32), squares, counts], axis=0)
 
-        def send_table(step, carry):
-            table_copy(level, target(plane - 1 - step), mine).start()
-            return carry
-
-        lax.fori_loop(0, plane - 1, send_table, 0)
+        for step in range(plane - 1, 0, -1):
+            table_copy(level, target(step), mine).start()
         return carry
 
     lax.fori_loop(0, depth, fit_level, 0)
     updates_ref[...] = tables[me, 0:params, :]
+
+    def drain(ref, semaphore):
+        pltpu.make_async_remote_copy(
+            src_ref=ref, dst_ref=ref, send_sem=semaphore, recv_sem=meta_recv_sem,
+            device_id=seat_coords(target(1)), device_id_type=MESH,
+        ).wait_send()
 
     def refit_level(level, tails):
         seats = pl.ds(0, plane - 1)
@@ -392,23 +403,18 @@
                 root_buf[row, :] = jnp.where(live, fresh, 0.0)
         return tails
 
-    tails = lax.fori_loop(0, depth, refit_level, jnp.zeros((2, LANES), jnp.float32))
+    tails = lax.fori_loop(0, depth - 1, refit_level, jnp.zeros((2, LANES), jnp.float32))
+    sent = depth * (plane - 1)
+    drain(out_buf.at[pl.ds(0, sent), pl.ds(0, words)], send_sem)
+    drain(meta_buf.at[others], meta_send_sem)
+    drain(sums_buf.at[others, :, pl.ds(0, used)], sums_send_sem)
+    tails = refit_level(depth - 1, tails)
     tails = jnp.sum(tails, axis=1, keepdims=True)
     norm = jnp.sqrt(jnp.maximum(tails[0:1], 0.0) / tails[1:2] + 1e-06)
     norm_ref[...] = jnp.broadcast_to(norm, norm_ref.shape)
     scale = 1.0 / norm
     fresh_ref[...] = root_buf[...] * scale
 
-    def drain(ref, semaphore):
-        pltpu.make_async_remote_copy(
-            src_ref=ref, dst_ref=ref, send_sem=semaphore, recv_sem=meta_recv_sem,
-            device_id=seat_coords(target(1)), device_id_type=MESH,
-        ).wait_send()
-
-    sent = depth * (plane - 1)
-    drain(out_buf.at[pl.ds(0, sent), pl.ds(0, words)], send_sem)
-    drain(meta_buf.at[others], meta_send_sem)
-    drain(sums_buf.at[others], sums_send_sem)
     drain(tables.at[pl.ds(0, sent)], table_send_sem)
 
 

time: 22.5 us -> 22.2 us (0.987)
  Pallas kernels: 21.6 us -> 21.3 us
    pallas_call x1, Pallas kernels: 21 us -> 20.7 us  [body(): pl.pallas_call(functools.partial(kernel, (groups, members, width, row_cou...]
where the time goes in v4:
time: 22.2 us; the launch traced here: 22 us
  Pallas kernels  21.3 us (96%)
  between operations  0.64 us (3%)
    pallas_call x1, Pallas kernels, body(): pl.pallas_call(functools.partial(kernel, (groups, members, width, row_cou...  20.7 us
    pallas_call x1, Pallas kernels, body(): pl.pallas_call(release, out_shape=tuple((jax.ShapeDtypeStruct(r.shape, r....  0.66 us

profile of v4, /device:TPU:0, one launch (start us, length us, event | category | flops | bytes accessed | tf_op | source)
XLA Modules:
  0.0 22.0 jit_solution(17358739496887628390)
XLA Ops:
  0.6 20.7 %exchange_fit.1 = (f32[5,128]{1,0:T(8,128)S(1)}, f32[128,128]{1,0:T(8,128)S(1)}, f32[1,128]{1,0:T(1,128)S(1)}) custom-call(s32[128,128]{1,0:T(8,128)} %bitcast.9, s32[128,128]{1,0:T(8,128)} %bitcast.10, s32[32,128]{1,0:T(8,128)} %bitcast.13, s32[1,128]{1,0:T(1,128)} %bitcast.14, f32[5,16384]{1,0:T(8,128)} %partials_hbm.1, f32[128,128]{1,0:T(8,128)} %bitcast.11, ...), custom_call_target="tpu_custom_call" | custom-call | tf_op jit(solution)/shard_map/exchange_fit/pallas_call | solution.py:463
  21.3 0.7 %release.1 = (f32[5,128]{1,0:T(8,128)}, f32[128,128]{1,0:T(8,128)}, f32[1,128]{1,0:T(1,128)}) custom-call(f32[5,128]{1,0:T(8,128)S(1)} %get-tuple-element.9.a_ref, f32[128,128]{1,0:T(8,128)S(1)} %get-tuple-element.10.b_ref, f32[1,128]{1,0:T(1,128)S(1)} %get-tuple-element.11.c_ref), custom_call_target="tpu_custom_call" | custom-call | tf_op jit(solution)/shard_map/release/pallas_call | solution.py:499

commit v5 on v4

--- a/solution.py
+++ b/solution.py
@@ -60,7 +60,7 @@
     updates_ref, fresh_ref, norm_ref,
     source_ref, slot_ref, owner_ref, counts_ref, partials_ref, residual_ref, weight_ref, prior_ref,
     root_buf, cell_buf, place_buf, out_buf, in_buf, meta_buf, first_buf, room_buf, sums_buf, tables,
-    load_sem, send_sem, recv_sem, meta_send_sem, meta_recv_sem, sums_send_sem, sums_recv_sem,
+    load_sem, send_sem, recv_sem, meta_send_sem, meta_recv_sem, meta_lead_sem, sums_send_sem, sums_recv_sem,
     table_send_sem, table_recv_sem,
 ):
     groups, members, width, pad_slots = sizes
@@ -99,24 +99,36 @@
         group, core = seat
         return (group, my_depth * CORES + core)
 
-    def level_coords(level):
-        return (my_group, level * CORES + my_core)
+    def level_coords(level, core=None):
+        return (my_group, level * CORES + (my_core if core is None else core))
+
+    lead = CORES - 1
 
     barrier = pltpu.get_barrier_semaphore()
     few = depth <= 4
     used = 3 * SUBLANES - 2
 
     def greet_level(step, carry):
-        pl.semaphore_signal(barrier, inc=1, device_id=level_coords((my_depth + step) % depth), device_id_type=MESH)
+        level = (my_depth + step) % depth
+        pl.semaphore_signal(barrier, inc=1, device_id=level_coords(level), device_id_type=MESH)
+        return carry
+
+    def greet_follower(step, carry):
+        level = (my_depth + step) % depth
+        pl.semaphore_signal(barrier, inc=1, device_id=level_coords(level, 0), device_id_type=MESH)
         return carry
 
     lax.fori_loop(1, depth, greet_level, 0, unroll=few)
+    lax.fori_loop(jnp.where(my_core == lead, 1, depth), depth, greet_follower, 0)
     for step in range(plane - 1, 0, -1):
         pl.semaphore_signal(barrier, inc=1, device_id=seat_coords(target(step)), device_id_type=MESH)
 
     for load in loads:
         load.wait()
 
+    meta_buf[my_core * depth + my_depth] = jnp.concatenate(
+        [prior_ref[...], counts_ref[...].astype(jnp.float32), jnp.zeros((SUBLANES - items, LANES), jnp.float32)], axis=0
+    )
     root = jnp.sqrt(weight_ref[...])
     root_buf[...] = root
     residual_ref[...] = residual_ref[...] * root
@@ -146,12 +158,13 @@
 
     prepare_level(0, 0)
 
-    pl.semaphore_wait(barrier, plane - 1 + depth - 1)
-
-    def meta_copy(level, slot):
+    pl.semaphore_wait(barrier, plane - 1 + (depth - 1) * (CORES - my_core))
+
+    def meta_copy(level, core, semaphore):
+        slot = my_core * depth + my_depth
         return pltpu.make_async_remote_copy(
-            src_ref=meta_buf.at[slot], dst_ref=meta_buf.at[slot], send_sem=meta_send_sem, recv_sem=meta_recv_sem,
-            device_id=level_coords(level), device_id_type=MESH,
+            src_ref=meta_buf.at[slot], dst_ref=meta_buf.at[slot], send_sem=meta_send_sem, recv_sem=semaphore,
+            device_id=level_coords(level, core), device_id_type=MESH,
         )
 
     def row_copy(level, seat, slot, part):
@@ -163,19 +176,31 @@
             device_id=seat_coords(seat), device_id_type=MESH,
         )
 
-    def sums_copy(level, stage, slot):
+    def sums_copy(level, stage):
+        slot = my_core * depth + my_depth
         return pltpu.make_async_remote_copy(
             src_ref=sums_buf.at[slot, stage, pl.ds(0, used)], dst_ref=sums_buf.at[slot, stage, pl.ds(0, used)],
             send_sem=sums_send_sem, recv_sem=sums_recv_sem.at[stage],
-            device_id=level_coords(level), device_id_type=MESH,
-        )
-
-    def table_copy(stage, seat, slot):
+            device_id=level_coords(level, lead), device_id_type=MESH,
+        )
+
+    def table_copy(stage, seat):
+        pair = pl.ds(my_group * members + stage * CORES, CORES)
         return pltpu.make_async_remote_copy(
-            src_ref=tables.at[slot], dst_ref=tables.at[slot],
+            src_ref=tables.at[pair], dst_ref=tables.at[pair],
             send_sem=table_send_sem, recv_sem=table_recv_sem.at[stage],
             device_id=seat_coords(seat), device_id_type=MESH,
         )
+
+    def send_meta(step, carry):
+        meta_copy((my_depth + step) % depth, my_core, meta_recv_sem).start()
+        return carry
+
+    def send_meta_lead(step, carry):
+        meta_copy((my_depth + step) % depth, lead, meta_lead_sem).start()
+        return carry
+
+    lax.fori_loop(1, depth, send_meta, 0, unroll=few)
 
     half = plane // 2
     batches = ([0] + list(range(plane - 1, half, -1)), list(range(half, 0, -1)))
@@ -193,6 +218,7 @@
 
     lax.fori_loop(1, depth, stream_rows, 0)
     send_rows(depth - 1)
+    lax.fori_loop(0, jnp.where(my_core == lead, 0, depth), send_meta_lead, 0)
 
     def own_rows(level, carry):
         in_buf[level, my_seat] = out_buf[my_group * members + level * CORES + my_core]
@@ -205,55 +231,23 @@
     row_index = lax.broadcasted_iota(jnp.int32, square, 0)
     lane_index = lax.broadcasted_iota(jnp.int32, square, 1)
     diagonal = row_index == lane_index
-
     spare = 4
 
-    def invert(step, total):
-        for part in range(spare):
-            tile = step * spare + part
-            ids = tile * LANES + lane_index
-            total = jnp.where(owner_ref[pl.ds(tile, 1), :] == row_index + me * src_local, ids, total)
-        return total
-
-    found = lax.fori_loop(0, owner_ref.shape[0] // spare, invert, jnp.zeros(square, jnp.int32))
-    source_at = jnp.sum(found.astype(jnp.float32), axis=1, keepdims=True)
-    source_at = jnp.sum(jnp.where(diagonal, source_at, 0.0), axis=0, keepdims=True)
-    meta_buf[my_depth] = jnp.concatenate(
-        [prior_ref[...], counts_ref[...].astype(jnp.float32), source_at * pad_slots]
-        + [jnp.zeros((SUBLANES - words, LANES), jnp.float32)],
-        axis=0,
-    )
-
-    def send_meta(step, carry):
-        meta_copy((my_depth + step) % depth, my_depth).start()
-        return carry
-
-    lax.fori_loop(1, depth, send_meta, 0)
-
-    batch = min(32, owner_ref.shape[0])
-
-    def locate(step, carry):
-        rows = pl.ds(pl.multiple_of(step * SUBLANES, SUBLANES), SUBLANES)
-        source = source_ref[rows, :]
-        lane, tile = source % LANES, source // LANES
-
-        def look(group, found):
-            for t in range(batch):
-                row = group * batch + t
-                entry = jnp.broadcast_to(owner_ref[pl.ds(row, 1), :], (SUBLANES, LANES))
-                found = jnp.where(tile == row, gather_lanes(entry, lane), found)
-            return found
-
-        found = jnp.full((SUBLANES, LANES), -1, jnp.int32)
-        if owner_ref.shape[0] == batch:
-            found = look(0, found)
-        else:
-            found = lax.fori_loop(0, owner_ref.shape[0] // batch, look, found)
-        place_buf[rows, :] = found % LANES
-        return carry
-
-    lax.fori_loop(0, source_ref.shape[0] // SUBLANES, locate, 0)
-
+    def invert(level, carry):
+        position = (my_group * members + level * CORES + my_core) * src_local + row_index
+
+        def scan(step, total):
+            for part in range(spare):
+                tile = step * spare + part
+                total = jnp.where(owner_ref[pl.ds(tile, 1), :] == position, tile * LANES + lane_index, total)
+            return total
+
+        found = lax.fori_loop(0, owner_ref.shape[0] // spare, scan, jnp.zeros(square, jnp.int32))
+        source_at = jnp.sum(found.astype(jnp.float32), axis=1, keepdims=True)
+        first_buf[level] = jnp.broadcast_to(source_at * pad_slots, square).astype(jnp.int32)
+        return carry
+
+    lax.fori_loop(0, depth, invert, 0)
 
     others = pl.ds(0, depth - 1)
     pltpu.make_async_remote_copy(
@@ -261,15 +255,13 @@
         device_id=level_coords((my_depth + 1) % depth), device_id_type=MESH,
     ).wait_recv()
 
-    def find_cells(level, carry):
-        first, counts = meta_buf[level, items:words, :], meta_buf[level, params:items, :]
-        first = jnp.sum(jnp.where(diagonal, first, 0.0), axis=1, keepdims=True)
+    def find_room(level, carry):
+        counts = meta_buf[my_core * depth + level, params:items, :]
         counts = jnp.sum(jnp.where(diagonal, counts, 0.0), axis=1, keepdims=True)
-        first_buf[level] = jnp.broadcast_to(first, square).astype(jnp.int32)
         room_buf[level] = jnp.broadcast_to(counts, square).astype(jnp.int32).astype(jnp.uint32)
         return carry
 
-    lax.fori_loop(0, depth, find_cells, 0, unroll=depth if depth <= 4 else 1)
+    lax.fori_loop(0, depth, find_room, 0, unroll=few)
     wide_sublane = lax.broadcasted_iota(jnp.int32, (SUBLANES, width), 0)
 
     low_rows = wide_sublane < 2
@@ -322,31 +314,65 @@
                 totals[lane] = part_sum if totals[lane] is None else totals[lane] + part_sum
         total = totals[0] - totals[1]
         total = total[0:height] + total[height : 2 * height] + total[2 * height : 3 * height]
-        sums_buf[my_depth, level] = total[0 : 3 * SUBLANES]
+        sums_buf[my_core * depth + my_depth, level] = total[0 : 3 * SUBLANES]
 
         def send_sums(step, carry):
-            sums_copy((my_depth + step) % depth, level, my_depth).start()
+            sums_copy((my_depth + step) % depth, level).start()
             return carry
 
-        lax.fori_loop(1, depth, send_sums, 0, unroll=few)
+        lax.fori_loop(jnp.where(my_core == lead, 1, 0), depth, send_sums, 0)
         return carry
 
     lax.fori_loop(0, depth, gather_level, 0)
+    batch = min(32, owner_ref.shape[0])
+
+    def locate(step, carry):
+        rows = pl.ds(pl.multiple_of(step * SUBLANES, SUBLANES), SUBLANES)
+        source = source_ref[rows, :]
+        lane, tile = source % LANES, source // LANES
+
+        def look(group, found):
+            for t in range(batch):
+                row = group * batch + t
+                entry = jnp.broadcast_to(owner_ref[pl.ds(row, 1), :], (SUBLANES, LANES))
+                found = jnp.where(tile == row, gather_lanes(entry, lane), found)
+            return found
+
+        found = jnp.full((SUBLANES, LANES), -1, jnp.int32)
+        if owner_ref.shape[0] == batch:
+            found = look(0, found)
+        else:
+            found = lax.fori_loop(0, owner_ref.shape[0] // batch, look, found)
+        place_buf[rows, :] = found % LANES
+        return carry
+
+    lax.fori_loop(0, source_ref.shape[0] // SUBLANES, locate, 0)
+
+
     at = {(0, 0): 0, (0, 1): 1, (0, 2): 2, (0, 3): 3, (0, 4): 4, (0, 5): 5, (5, 5): 6,
           (3, 5): 8, (1, 1): 9, (1, 2): 10, (1, 3): 11, (1, 4): 12, (1, 5): 13, (3, 3): 14, (3, 4): 15,
           (4, 4): 16, (4, 5): 17, (2, 2): 18, (2, 3): 19, (2, 4): 20, (2, 5): 21}
 
+    senders = pl.ds(0, CORES * depth - 1)
+
     def fit_level(level, carry):
         pltpu.make_async_remote_copy(
-            src_ref=sums_buf.at[others, level, pl.ds(0, used)], dst_ref=sums_buf.at[others, level, pl.ds(0, used)],
+            src_ref=sums_buf.at[senders, level, pl.ds(0, used)], dst_ref=sums_buf.at[senders, level, pl.ds(0, used)],
             send_sem=sums_send_sem, recv_sem=sums_recv_sem.at[level],
             device_id=level_coords((my_depth + 1) % depth), device_id_type=MESH,
         ).wait_recv()
-
+        for core in range(CORES):
+            fit(level, core)
+        for step in range(plane - 1, 0, -1):
+            table_copy(level, target(step)).start()
+        return carry
+
+    def fit(level, core):
         def gather_sums(slot, total):
-            return total + sums_buf[slot, level, 0:used, :]
-
-        total = lax.fori_loop(1, depth, gather_sums, sums_buf[0, level, 0:used, :], unroll=few)
+            return total + sums_buf[core * depth + slot, level, 0:used, :]
+
+        total = lax.fori_loop(1, depth, gather_sums, sums_buf[core * depth, level, 0:used, :], unroll=few)
+        meta = meta_buf[core * depth + level]
 
         def entry(i, j):
             spot = at[min(i, j), max(i, j)]
@@ -356,7 +382,7 @@
         moments = [entry(i, params) for i in range(params)]
         with_prior = [[normal[i][j] for j in range(params)] for i in range(params)]
         for i in range(params):
-            with_prior[i][i] = normal[i][i] + meta_buf[level, i : i + 1, :]
+            with_prior[i][i] = normal[i][i] + meta[i : i + 1, :]
         updates = solve_rows(with_prior, moments)
         squares = entry(params, params)
         for i in range(params):
@@ -364,16 +390,19 @@
             for j in range(1, params):
                 fitted = fitted + normal[i][j] * updates[j]
             squares = squares + updates[i] * (fitted - 2.0 * moments[i])
-        counts = meta_buf[level, params:items, :]
-        mine = my_group * members + level * CORES + my_core
-        tables[mine] = jnp.concatenate(updates + [jnp.full((1, LANES), -1.0, jnp.float32), squares, counts], axis=0)
-
-        for step in range(plane - 1, 0, -1):
-            table_copy(level, target(step), mine).start()
-        return carry
-
-    lax.fori_loop(0, depth, fit_level, 0)
-    updates_ref[...] = tables[me, 0:params, :]
+        minus = jnp.full((1, LANES), -1.0, jnp.float32)
+        tables[my_group * members + level * CORES + core] = jnp.concatenate(
+            updates + [minus, squares, meta[params:items, :]], axis=0
+        )
+
+    @pl.when(my_core == lead)
+    def lead_fits():
+        pltpu.make_async_remote_copy(
+            src_ref=meta_buf.at[pl.ds(0, depth)], dst_ref=meta_buf.at[pl.ds(0, depth)],
+            send_sem=meta_send_sem, recv_sem=meta_lead_sem, device_id=level_coords(my_depth, 0), device_id_type=MESH,
+        ).wait_recv()
+        lax.fori_loop(0, depth, fit_level, 0)
+
 
     def drain(ref, semaphore):
         pltpu.make_async_remote_copy(
@@ -382,12 +411,21 @@
         ).wait_send()
 
     def refit_level(level, tails):
-        seats = pl.ds(0, plane - 1)
-        pltpu.make_async_remote_copy(
-            src_ref=tables.at[seats], dst_ref=tables.at[seats],
-            send_sem=table_send_sem, recv_sem=table_recv_sem.at[level],
-            device_id=seat_coords(target(1)), device_id_type=MESH,
-        ).wait_recv()
+        def await_tables(count):
+            pairs = pl.ds(0, count * CORES)
+            pltpu.make_async_remote_copy(
+                src_ref=tables.at[pairs], dst_ref=tables.at[pairs],
+                send_sem=table_send_sem, recv_sem=table_recv_sem.at[level],
+                device_id=seat_coords(target(1)), device_id_type=MESH,
+            ).wait_recv()
+
+        @pl.when(my_core == lead)
+        def await_leads():
+            await_tables(groups - 1)
+
+        @pl.when(my_core != lead)
+        def await_all():
+            await_tables(groups)
 
         for seat in range(plane):
             k = seat // CORES * members + level * CORES + seat % CORES
@@ -406,16 +444,32 @@
     tails = lax.fori_loop(0, depth - 1, refit_level, jnp.zeros((2, LANES), jnp.float32))
     sent = depth * (plane - 1)
     drain(out_buf.at[pl.ds(0, sent), pl.ds(0, words)], send_sem)
-    drain(meta_buf.at[others], meta_send_sem)
-    drain(sums_buf.at[others, :, pl.ds(0, used)], sums_send_sem)
+
+    @pl.when(my_core == lead)
+    def drain_lead():
+        drain(meta_buf.at[pl.ds(0, depth - 1)], meta_send_sem)
+        drain(sums_buf.at[pl.ds(0, depth - 1), :, pl.ds(0, used)], sums_send_sem)
+
+    @pl.when(my_core != lead)
+    def drain_follower():
+        drain(meta_buf.at[pl.ds(0, CORES * depth - 1)], meta_send_sem)
+        drain(sums_buf.at[pl.ds(0, depth), :, pl.ds(0, used)], sums_send_sem)
+
     tails = refit_level(depth - 1, tails)
     tails = jnp.sum(tails, axis=1, keepdims=True)
+    updates_ref[...] = tables[me, 0:params, :]
     norm = jnp.sqrt(jnp.maximum(tails[0:1], 0.0) / tails[1:2] + 1e-06)
     norm_ref[...] = jnp.broadcast_to(norm, norm_ref.shape)
     scale = 1.0 / norm
     fresh_ref[...] = root_buf[...] * scale
 
-    drain(tables.at[pl.ds(0, sent)], table_send_sem)
+    @pl.when(my_core == lead)
+    def drain_tables():
+        def drain_seat(step, carry):
+            drain(tables.at[pl.ds(0, depth * CORES)], table_send_sem)
+            return carry
+
+        lax.fori_loop(1, plane, drain_seat, 0)
 
 
 def release(a_ref, b_ref, c_ref, a_out, b_out, c_out, sem):
@@ -475,14 +529,15 @@
             pltpu.VMEM((rows, LANES), jnp.int32),
             pltpu.VMEM((n, SUBLANES, width), jnp.float32),
             pltpu.VMEM((depth, plane, SUBLANES, width), jnp.float32),
-            pltpu.VMEM((depth, SUBLANES, LANES), jnp.float32),
+            pltpu.VMEM((CORES * depth, SUBLANES, LANES), jnp.float32),
             pltpu.VMEM((depth, src_local, LANES), jnp.int32),
             pltpu.VMEM((depth, src_local, LANES), jnp.uint32),
-            pltpu.VMEM((depth, depth, 3 * SUBLANES, LANES), jnp.float32),
+            pltpu.VMEM((CORES * depth, depth, 3 * SUBLANES, LANES), jnp.float32),
             pltpu.VMEM((n, SUBLANES, LANES), jnp.float32),
             pltpu.SemaphoreType.DMA((len(operands),)),
             pltpu.SemaphoreType.DMA,
             pltpu.SemaphoreType.DMA((depth, 2)),
+            pltpu.SemaphoreType.DMA,
             pltpu.SemaphoreType.DMA,
             pltpu.SemaphoreType.DMA,
             pltpu.SemaphoreType.DMA,

time: 22.2 us -> 21.4 us (0.964)
  Pallas kernels: 21.3 us -> 20.5 us
    pallas_call x1, Pallas kernels: 20.7 us -> 19.8 us  [body(): pl.pallas_call(functools.partial(kernel, (groups, members, width, row_cou...]
where the time goes in v5:
time: 21.4 us; the launch traced here: 21.2 us
  Pallas kernels  20.5 us (96%)
  between operations  0.64 us (3%)
    pallas_call x1, Pallas kernels, body(): pl.pallas_call(functools.partial(kernel, (groups, members, width, row_cou...  19.8 us
    pallas_call x1, Pallas kernels, body(): pl.pallas_call(release, out_shape=tuple((jax.ShapeDtypeStruct(r.shape, r....  0.66 us

profile of v5, /device:TPU:0, one launch (start us, length us, event | category | flops | bytes accessed | tf_op | source)
XLA Modules:
  0.0 21.2 jit_solution(10789130817341276216)
XLA Ops:
  0.6 19.8 %exchange_fit.1 = (f32[5,128]{1,0:T(8,128)S(1)}, f32[128,128]{1,0:T(8,128)S(1)}, f32[1,128]{1,0:T(1,128)S(1)}) custom-call(s32[128,128]{1,0:T(8,128)} %bitcast.9, s32[128,128]{1,0:T(8,128)} %bitcast.10, s32[32,128]{1,0:T(8,128)} %bitcast.13, s32[1,128]{1,0:T(1,128)} %bitcast.14, f32[5,16384]{1,0:T(8,128)} %partials_hbm.1, f32[128,128]{1,0:T(8,128)} %bitcast.11, ...), custom_call_target="tpu_custom_call" | custom-call | tf_op jit(solution)/shard_map/exchange_fit/pallas_call | solution.py:517
  20.5 0.7 %release.1 = (f32[5,128]{1,0:T(8,128)}, f32[128,128]{1,0:T(8,128)}, f32[1,128]{1,0:T(1,128)}) custom-call(f32[5,128]{1,0:T(8,128)S(1)} %get-tuple-element.9.a_ref, f32[128,128]{1,0:T(8,128)S(1)} %get-tuple-element.10.b_ref, f32[1,128]{1,0:T(1,128)S(1)} %get-tuple-element.11.c_ref), custom_call_target="tpu_custom_call" | custom-call | tf_op jit(solution)/shard_map/release/pallas_call | solution.py:554

commit v6 on v5

--- a/solution.py
+++ b/solution.py
@@ -60,7 +60,7 @@
     updates_ref, fresh_ref, norm_ref,
     source_ref, slot_ref, owner_ref, counts_ref, partials_ref, residual_ref, weight_ref, prior_ref,
     root_buf, cell_buf, place_buf, out_buf, in_buf, meta_buf, first_buf, room_buf, sums_buf, tables,
-    load_sem, send_sem, recv_sem, meta_send_sem, meta_recv_sem, meta_lead_sem, sums_send_sem, sums_recv_sem,
+    load_sem, send_sem, recv_sem, meta_send_sem, meta_recv_sem, sums_send_sem, sums_recv_sem,
     table_send_sem, table_recv_sem,
 ):
     groups, members, width, pad_slots = sizes
@@ -104,22 +104,30 @@
 
     lead = CORES - 1
 
+    def unit_of(index):
+        return index // CORES * CORES + my_core, index % CORES
+
+    def home_of(level, core):
+        return level % CORES, level // CORES * CORES + core
+
+    def far_first(step):
+        return jnp.where(my_depth < depth // 2, depth - 1 - step, step)
+
     barrier = pltpu.get_barrier_semaphore()
     few = depth <= 4
     used = 3 * SUBLANES - 2
 
     def greet_level(step, carry):
-        level = (my_depth + step) % depth
-        pl.semaphore_signal(barrier, inc=1, device_id=level_coords(level), device_id_type=MESH)
-        return carry
-
-    def greet_follower(step, carry):
-        level = (my_depth + step) % depth
-        pl.semaphore_signal(barrier, inc=1, device_id=level_coords(level, 0), device_id_type=MESH)
-        return carry
-
-    lax.fori_loop(1, depth, greet_level, 0, unroll=few)
-    lax.fori_loop(jnp.where(my_core == lead, 1, depth), depth, greet_follower, 0)
+        level = far_first(step)
+
+        @pl.when(level != my_depth)
+        def greet():
+            for core in range(CORES):
+                pl.semaphore_signal(barrier, inc=1, device_id=level_coords(level, core), device_id_type=MESH)
+
+        return carry
+
+    lax.fori_loop(0, depth, greet_level, 0, unroll=few)
     for step in range(plane - 1, 0, -1):
         pl.semaphore_signal(barrier, inc=1, device_id=seat_coords(target(step)), device_id_type=MESH)
 
@@ -158,26 +166,27 @@
 
     prepare_level(0, 0)
 
-    pl.semaphore_wait(barrier, plane - 1 + (depth - 1) * (CORES - my_core))
-
-    def meta_copy(level, core, semaphore):
+    pl.semaphore_wait(barrier, plane - 1 + CORES * (depth - 1))
+
+    def meta_copy(level, core):
         slot = my_core * depth + my_depth
         return pltpu.make_async_remote_copy(
-            src_ref=meta_buf.at[slot], dst_ref=meta_buf.at[slot], send_sem=meta_send_sem, recv_sem=semaphore,
+            src_ref=meta_buf.at[slot], dst_ref=meta_buf.at[slot], send_sem=meta_send_sem, recv_sem=meta_recv_sem,
             device_id=level_coords(level, core), device_id_type=MESH,
         )
 
-    def row_copy(level, seat, slot, part):
-        group, core = seat
+    def row_copy(level, core, jump, part):
+        home, unit = home_of(level, core)
+        group, _ = target(jump * CORES)
         return pltpu.make_async_remote_copy(
             src_ref=out_buf.at[group * members + level * CORES + core, pl.ds(0, words)],
-            dst_ref=in_buf.at[level, slot, pl.ds(0, words)],
-            send_sem=send_sem, recv_sem=recv_sem.at[level, part],
-            device_id=seat_coords(seat), device_id_type=MESH,
-        )
-
-    def sums_copy(level, stage):
-        slot = my_core * depth + my_depth
+            dst_ref=in_buf.at[unit, my_seat, pl.ds(0, words)],
+            send_sem=send_sem, recv_sem=recv_sem.at[unit, part],
+            device_id=seat_coords((group, home)), device_id_type=MESH,
+        )
+
+    def sums_copy(level, stage, core):
+        slot = core * depth + my_depth
         return pltpu.make_async_remote_copy(
             src_ref=sums_buf.at[slot, stage, pl.ds(0, used)], dst_ref=sums_buf.at[slot, stage, pl.ds(0, used)],
             send_sem=sums_send_sem, recv_sem=sums_recv_sem.at[stage],
@@ -193,23 +202,22 @@
         )
 
     def send_meta(step, carry):
-        meta_copy((my_depth + step) % depth, my_core, meta_recv_sem).start()
-        return carry
-
-    def send_meta_lead(step, carry):
-        meta_copy((my_depth + step) % depth, lead, meta_lead_sem).start()
-        return carry
-
-    lax.fori_loop(1, depth, send_meta, 0, unroll=few)
-
-    half = plane // 2
-    batches = ([0] + list(range(plane - 1, half, -1)), list(range(half, 0, -1)))
+        level = far_first(step)
+        for core in range(CORES):
+            pl.when(jnp.logical_or(level != my_depth, my_core != core))(meta_copy(level, core).start)
+        return carry
+
+    lax.fori_loop(0, depth, send_meta, 0, unroll=few)
+    batches = ([0] + list(range(groups - 1, groups // 2, -1)), list(range(groups // 2, 0, -1)))
 
     def send_rows(level):
-        for part, steps in enumerate(batches):
-            for step in steps:
-                if step:
-                    row_copy(level, target(step), my_seat, part).start()
+        for core in range(CORES):
+            for jump in range(groups - 1, -1, -1):
+                copy = row_copy(level, core, jump, int(jump in batches[1]))
+                if jump:
+                    copy.start()
+                else:
+                    pl.when(home_of(level, core)[0] != my_core)(copy.start)
 
     def stream_rows(level, carry):
         prepare_level(level, 0)
@@ -218,10 +226,10 @@
 
     lax.fori_loop(1, depth, stream_rows, 0)
     send_rows(depth - 1)
-    lax.fori_loop(0, jnp.where(my_core == lead, 0, depth), send_meta_lead, 0)
-
-    def own_rows(level, carry):
-        in_buf[level, my_seat] = out_buf[my_group * members + level * CORES + my_core]
+
+    def own_rows(unit, carry):
+        level, core = unit_of(unit)
+        in_buf[unit, my_seat] = out_buf[my_group * members + level * CORES + core]
         return carry
 
     lax.fori_loop(0, depth, own_rows, 0)
@@ -233,8 +241,9 @@
     diagonal = row_index == lane_index
     spare = 4
 
-    def invert(level, carry):
-        position = (my_group * members + level * CORES + my_core) * src_local + row_index
+    def invert(unit, carry):
+        level, core = unit_of(unit)
+        position = (my_group * members + level * CORES + core) * src_local + row_index
 
         def scan(step, total):
             for part in range(spare):
@@ -244,21 +253,22 @@
 
         found = lax.fori_loop(0, owner_ref.shape[0] // spare, scan, jnp.zeros(square, jnp.int32))
         source_at = jnp.sum(found.astype(jnp.float32), axis=1, keepdims=True)
-        first_buf[level] = jnp.broadcast_to(source_at * pad_slots, square).astype(jnp.int32)
+        first_buf[unit] = jnp.broadcast_to(source_at * pad_slots, square).astype(jnp.int32)
         return carry
 
     lax.fori_loop(0, depth, invert, 0)
 
-    others = pl.ds(0, depth - 1)
+    others = pl.ds(0, CORES * depth - 1)
     pltpu.make_async_remote_copy(
         src_ref=meta_buf.at[others], dst_ref=meta_buf.at[others], send_sem=meta_send_sem, recv_sem=meta_recv_sem,
         device_id=level_coords((my_depth + 1) % depth), device_id_type=MESH,
     ).wait_recv()
 
-    def find_room(level, carry):
-        counts = meta_buf[my_core * depth + level, params:items, :]
+    def find_room(unit, carry):
+        level, core = unit_of(unit)
+        counts = meta_buf[core * depth + level, params:items, :]
         counts = jnp.sum(jnp.where(diagonal, counts, 0.0), axis=1, keepdims=True)
-        room_buf[level] = jnp.broadcast_to(counts, square).astype(jnp.int32).astype(jnp.uint32)
+        room_buf[unit] = jnp.broadcast_to(counts, square).astype(jnp.int32).astype(jnp.uint32)
         return carry
 
     lax.fori_loop(0, depth, find_room, 0, unroll=few)
@@ -268,16 +278,16 @@
     sixth_row = wide_sublane == items
     outer_rows = jnp.logical_or(wide_sublane == 0, wide_sublane >= items)
 
-    def absorb(level, slot, sign):
-        first_cell, room = first_buf[level], room_buf[level]
-        rows = in_buf[level, slot]
+    def absorb(unit, slot, sign):
+        first_cell, room = first_buf[unit], room_buf[unit]
+        rows = in_buf[unit, slot]
 
         def spread(i):
-            return jnp.broadcast_to(in_buf[level, slot, i : i + 1, :], (SUBLANES, width))
+            return jnp.broadcast_to(in_buf[unit, slot, i : i + 1, :], (SUBLANES, width))
 
         hot = []
         for piece in range(pieces):
-            part = in_buf[level, slot, items:words, piece * LANES : (piece + 1) * LANES].astype(jnp.int32)
+            part = in_buf[unit, slot, items:words, piece * LANES : (piece + 1) * LANES].astype(jnp.int32)
             hit = (part - first_cell).astype(jnp.uint32) < room
             hot.append(jnp.where(hit, sign, 0.0))
         hot = jnp.concatenate(hot, axis=1).astype(jnp.bfloat16)
@@ -296,34 +306,34 @@
 
     height = 4 * SUBLANES
 
-    def gather_level(level, carry):
+    def gather_unit(unit, carry):
+        level, owner_core = unit_of(unit)
         totals = [None, None]
-        for part, steps in enumerate(batches):
-            def batch_rows(count):
-                return in_buf.at[level, pl.ds(0, count), pl.ds(0, words)]
-
-            count = len([step for step in steps if step])
+        for part, jumps in enumerate(batches):
+            count = CORES * len(jumps) - (part == 0)
+            block = in_buf.at[unit, pl.ds(0, count), pl.ds(0, words)]
             pltpu.make_async_remote_copy(
-                src_ref=batch_rows(count), dst_ref=batch_rows(count), send_sem=send_sem,
-                recv_sem=recv_sem.at[level, part], device_id=seat_coords(target(1)), device_id_type=MESH,
+                src_ref=block, dst_ref=block, send_sem=send_sem, recv_sem=recv_sem.at[unit, part],
+                device_id=seat_coords(target(1)), device_id_type=MESH,
             ).wait_recv()
-            for spot, step in enumerate(steps):
-                group, core = origin(step)
-                lane = spot % 2
-                part_sum = absorb(level, group * CORES + core, 1.0 - 2.0 * lane)
-                totals[lane] = part_sum if totals[lane] is None else totals[lane] + part_sum
+            for jump in jumps:
+                group, _ = origin(jump * CORES)
+                for core in range(CORES):
+                    part_sum = absorb(unit, group * CORES + core, 1.0 - 2.0 * core)
+                    totals[core] = part_sum if totals[core] is None else totals[core] + part_sum
         total = totals[0] - totals[1]
         total = total[0:height] + total[height : 2 * height] + total[2 * height : 3 * height]
-        sums_buf[my_core * depth + my_depth, level] = total[0 : 3 * SUBLANES]
+        sums_buf[owner_core * depth + my_depth, level] = total[0 : 3 * SUBLANES]
 
         def send_sums(step, carry):
-            sums_copy((my_depth + step) % depth, level).start()
+            aim = far_first(step)
+            pl.when(jnp.logical_or(aim != my_depth, my_core != lead))(sums_copy(aim, level, owner_core).start)
             return carry
 
-        lax.fori_loop(jnp.where(my_core == lead, 1, 0), depth, send_sums, 0)
-        return carry
-
-    lax.fori_loop(0, depth, gather_level, 0)
+        lax.fori_loop(0, depth, send_sums, 0, unroll=few)
+        return carry
+
+    lax.fori_loop(0, depth, gather_unit, 0)
     batch = min(32, owner_ref.shape[0])
 
     def locate(step, carry):
@@ -353,19 +363,16 @@
           (3, 5): 8, (1, 1): 9, (1, 2): 10, (1, 3): 11, (1, 4): 12, (1, 5): 13, (3, 3): 14, (3, 4): 15,
           (4, 4): 16, (4, 5): 17, (2, 2): 18, (2, 3): 19, (2, 4): 20, (2, 5): 21}
 
-    senders = pl.ds(0, CORES * depth - 1)
-
-    def fit_level(level, carry):
+    def fit_level(level, count):
+        block = sums_buf.at[pl.ds(0, count), level, pl.ds(0, used)]
         pltpu.make_async_remote_copy(
-            src_ref=sums_buf.at[senders, level, pl.ds(0, used)], dst_ref=sums_buf.at[senders, level, pl.ds(0, used)],
-            send_sem=sums_send_sem, recv_sem=sums_recv_sem.at[level],
+            src_ref=block, dst_ref=block, send_sem=sums_send_sem, recv_sem=sums_recv_sem.at[level],
             device_id=level_coords((my_depth + 1) % depth), device_id_type=MESH,
         ).wait_recv()
         for core in range(CORES):
             fit(level, core)
         for step in range(plane - 1, 0, -1):
             table_copy(level, target(step)).start()
-        return carry
 
     def fit(level, core):
         def gather_sums(slot, total):
@@ -397,12 +404,12 @@
 
     @pl.when(my_core == lead)
     def lead_fits():
-        pltpu.make_async_remote_copy(
-            src_ref=meta_buf.at[pl.ds(0, depth)], dst_ref=meta_buf.at[pl.ds(0, depth)],
-            send_sem=meta_send_sem, recv_sem=meta_lead_sem, device_id=level_coords(my_depth, 0), device_id_type=MESH,
-        ).wait_recv()
-        lax.fori_loop(0, depth, fit_level, 0)
-
+        def fit_pair(step, carry):
+            for core in range(CORES):
+                fit_level(step * CORES + core, CORES * (depth - (core == lead)))
+            return carry
+
+        lax.fori_loop(0, depth // CORES, fit_pair, 0)
 
     def drain(ref, semaphore):
         pltpu.make_async_remote_copy(
@@ -444,15 +451,14 @@
     tails = lax.fori_loop(0, depth - 1, refit_level, jnp.zeros((2, LANES), jnp.float32))
     sent = depth * (plane - 1)
     drain(out_buf.at[pl.ds(0, sent), pl.ds(0, words)], send_sem)
+    drain(meta_buf.at[others], meta_send_sem)
 
     @pl.when(my_core == lead)
     def drain_lead():
-        drain(meta_buf.at[pl.ds(0, depth - 1)], meta_send_sem)
         drain(sums_buf.at[pl.ds(0, depth - 1), :, pl.ds(0, used)], sums_send_sem)
 
     @pl.when(my_core != lead)
     def drain_follower():
-        drain(meta_buf.at[pl.ds(0, CORES * depth - 1)], meta_send_sem)
         drain(sums_buf.at[pl.ds(0, depth), :, pl.ds(0, used)], sums_send_sem)
 
     tails = refit_level(depth - 1, tails)
@@ -540,7 +546,6 @@
             pltpu.SemaphoreType.DMA,
             pltpu.SemaphoreType.DMA,
             pltpu.SemaphoreType.DMA,
-            pltpu.SemaphoreType.DMA,
             pltpu.SemaphoreType.DMA((depth,)),
             pltpu.SemaphoreType.DMA,
             pltpu.SemaphoreType.DMA((depth,)),

time: 21.4 us -> 21.2 us (level)
  no operation moved by 1% of the time
where the time goes in v6:
time: 21.2 us; the launch traced here: 21 us
  Pallas kernels  20.3 us (96%)
  between operations  0.64 us (3%)
    pallas_call x1, Pallas kernels, body(): pl.pallas_call(functools.partial(kernel, (groups, members, width, row_cou...  19.7 us
    pallas_call x1, Pallas kernels, body(): pl.pallas_call(release, out_shape=tuple((jax.ShapeDtypeStruct(r.shape, r....  0.66 us

profile of v6, /device:TPU:0, one launch (start us, length us, event | category | flops | bytes accessed | tf_op | source)
XLA Modules:
  0.0 21.0 jit_solution(12053070809377176499)
XLA Ops:
  0.6 19.7 %exchange_fit.1 = (f32[5,128]{1,0:T(8,128)S(1)}, f32[128,128]{1,0:T(8,128)S(1)}, f32[1,128]{1,0:T(1,128)S(1)}) custom-call(s32[128,128]{1,0:T(8,128)} %bitcast.9, s32[128,128]{1,0:T(8,128)} %bitcast.10, s32[32,128]{1,0:T(8,128)} %bitcast.13, s32[1,128]{1,0:T(1,128)} %bitcast.14, f32[5,16384]{1,0:T(8,128)} %partials_hbm.1, f32[128,128]{1,0:T(8,128)} %bitcast.11, ...), custom_call_target="tpu_custom_call" | custom-call | tf_op jit(solution)/shard_map/exchange_fit/pallas_call | solution.py:523
  20.3 0.7 %release.1 = (f32[5,128]{1,0:T(8,128)}, f32[128,128]{1,0:T(8,128)}, f32[1,128]{1,0:T(1,128)}) custom-call(f32[5,128]{1,0:T(8,128)S(1)} %get-tuple-element.9.a_ref, f32[128,128]{1,0:T(8,128)S(1)} %get-tuple-element.10.b_ref, f32[1,128]{1,0:T(1,128)S(1)} %get-tuple-element.11.c_ref), custom_call_target="tpu_custom_call" | custom-call | tf_op jit(solution)/shard_map/release/pallas_call | solution.py:559

commit v7 on v6

--- a/solution.py
+++ b/solution.py
@@ -61,7 +61,7 @@
     source_ref, slot_ref, owner_ref, counts_ref, partials_ref, residual_ref, weight_ref, prior_ref,
     root_buf, cell_buf, place_buf, out_buf, in_buf, meta_buf, first_buf, room_buf, sums_buf, tables,
     load_sem, send_sem, recv_sem, meta_send_sem, meta_recv_sem, sums_send_sem, sums_recv_sem,
-    table_send_sem, table_recv_sem,
+    table_send_sem, table_recv_sem, gate_sem,
 ):
     groups, members, width, pad_slots = sizes
     n = groups * members
@@ -104,11 +104,15 @@
 
     lead = CORES - 1
 
+    def level_at(turn):
+        return depth - 1 - turn
+
     def unit_of(index):
-        return index // CORES * CORES + my_core, index % CORES
+        return level_at(index // CORES * CORES + my_core), index % CORES
 
     def home_of(level, core):
-        return level % CORES, level // CORES * CORES + core
+        turn = depth - 1 - level
+        return turn % CORES, turn // CORES * CORES + core
 
     def far_first(step):
         return jnp.where(my_depth < depth // 2, depth - 1 - step, step)
@@ -117,19 +121,18 @@
     few = depth <= 4
     used = 3 * SUBLANES - 2
 
+    def tell(semaphore, level):
+        for core in range(CORES):
+            pl.semaphore_signal(semaphore, inc=1, device_id=level_coords(level, core), device_id_type=MESH)
+
     def greet_level(step, carry):
-        level = far_first(step)
-
-        @pl.when(level != my_depth)
-        def greet():
-            for core in range(CORES):
-                pl.semaphore_signal(barrier, inc=1, device_id=level_coords(level, core), device_id_type=MESH)
-
-        return carry
-
-    lax.fori_loop(0, depth, greet_level, 0, unroll=few)
+        level = level_at(step)
+        pl.when(level > my_depth)(lambda: tell(barrier, level))
+        return carry
+
     for step in range(plane - 1, 0, -1):
         pl.semaphore_signal(barrier, inc=1, device_id=seat_coords(target(step)), device_id_type=MESH)
+    lax.fori_loop(0, depth, greet_level, 0, unroll=few)
 
     for load in loads:
         load.wait()
@@ -164,15 +167,15 @@
     def prepare_level(level, carry):
         return lax.fori_loop(0, plane, functools.partial(prepare, level), carry, unroll=2)
 
-    prepare_level(0, 0)
-
-    pl.semaphore_wait(barrier, plane - 1 + CORES * (depth - 1))
+    prepare_level(level_at(0), 0)
+
+    pl.semaphore_wait(barrier, plane - 1 + CORES * my_depth)
 
     def meta_copy(level, core):
         slot = my_core * depth + my_depth
         return pltpu.make_async_remote_copy(
-            src_ref=meta_buf.at[slot], dst_ref=meta_buf.at[slot], send_sem=meta_send_sem, recv_sem=meta_recv_sem,
-            device_id=level_coords(level, core), device_id_type=MESH,
+            src_ref=meta_buf.at[slot], dst_ref=meta_buf.at[slot], send_sem=meta_send_sem,
+            recv_sem=meta_recv_sem.at[my_depth], device_id=level_coords(level, core), device_id_type=MESH,
         )
 
     def row_copy(level, core, jump, part):
@@ -201,13 +204,20 @@
             device_id=seat_coords(seat), device_id_type=MESH,
         )
 
-    def send_meta(step, carry):
-        level = far_first(step)
+    def send_meta_down(level, carry):
         for core in range(CORES):
-            pl.when(jnp.logical_or(level != my_depth, my_core != core))(meta_copy(level, core).start)
-        return carry
-
-    lax.fori_loop(0, depth, send_meta, 0, unroll=few)
+            remote = jnp.logical_or(level < my_depth, jnp.logical_and(level == my_depth, my_core != core))
+            pl.when(remote)(meta_copy(level, core).start)
+        pl.when(level < my_depth)(lambda: tell(gate_sem, level))
+        return carry
+
+    def send_meta_up(step, carry):
+        level = level_at(step)
+        for core in range(CORES):
+            pl.when(level > my_depth)(meta_copy(level, core).start)
+        return carry
+
+    lax.fori_loop(0, depth, send_meta_down, 0, unroll=few)
     batches = ([0] + list(range(groups - 1, groups // 2, -1)), list(range(groups // 2, 0, -1)))
 
     def send_rows(level):
@@ -219,13 +229,13 @@
                 else:
                     pl.when(home_of(level, core)[0] != my_core)(copy.start)
 
-    def stream_rows(level, carry):
-        prepare_level(level, 0)
-        send_rows(level - 1)
+    def stream_rows(turn, carry):
+        prepare_level(level_at(turn), 0)
+        send_rows(level_at(turn - 1))
         return carry
 
     lax.fori_loop(1, depth, stream_rows, 0)
-    send_rows(depth - 1)
+    send_rows(level_at(depth - 1))
 
     def own_rows(unit, carry):
         level, core = unit_of(unit)
@@ -258,11 +268,48 @@
 
     lax.fori_loop(0, depth, invert, 0)
 
+    @pl.when(my_depth < depth - 1)
+    def open_up():
+        pl.semaphore_wait(gate_sem, CORES * (depth - 1 - my_depth))
+        lax.fori_loop(0, depth, send_meta_up, 0, unroll=few)
+
+    batch = min(32, owner_ref.shape[0])
+
+    def locate(step, carry):
+        rows = pl.ds(pl.multiple_of(step * SUBLANES, SUBLANES), SUBLANES)
+        source = source_ref[rows, :]
+        lane, tile = source % LANES, source // LANES
+
+        def look(group, found):
+            for t in range(batch):
+                row = group * batch + t
+                entry = jnp.broadcast_to(owner_ref[pl.ds(row, 1), :], (SUBLANES, LANES))
+                found = jnp.where(tile == row, gather_lanes(entry, lane), found)
+            return found
+
+        found = jnp.full((SUBLANES, LANES), -1, jnp.int32)
+        if owner_ref.shape[0] == batch:
+            found = look(0, found)
+        else:
+            found = lax.fori_loop(0, owner_ref.shape[0] // batch, look, found)
+        place_buf[rows, :] = found % LANES
+        return carry
+
+    lax.fori_loop(0, source_ref.shape[0] // SUBLANES, locate, 0)
+
+
     others = pl.ds(0, CORES * depth - 1)
-    pltpu.make_async_remote_copy(
-        src_ref=meta_buf.at[others], dst_ref=meta_buf.at[others], send_sem=meta_send_sem, recv_sem=meta_recv_sem,
-        device_id=level_coords((my_depth + 1) % depth), device_id_type=MESH,
-    ).wait_recv()
+
+    def await_meta(level):
+        def take(count):
+            block = meta_buf.at[pl.ds(0, count)]
+            pltpu.make_async_remote_copy(
+                src_ref=block, dst_ref=block, send_sem=meta_send_sem, recv_sem=meta_recv_sem.at[level],
+                device_id=seat_coords(target(1)), device_id_type=MESH,
+            ).wait_recv()
+
+        pl.when(level == my_depth)(lambda: take(CORES - 1))
+        pl.when(level != my_depth)(lambda: take(CORES))
 
     def find_room(unit, carry):
         level, core = unit_of(unit)
@@ -271,7 +318,6 @@
         room_buf[unit] = jnp.broadcast_to(counts, square).astype(jnp.int32).astype(jnp.uint32)
         return carry
 
-    lax.fori_loop(0, depth, find_room, 0, unroll=few)
     wide_sublane = lax.broadcasted_iota(jnp.int32, (SUBLANES, width), 0)
 
     low_rows = wide_sublane < 2
@@ -333,32 +379,17 @@
         lax.fori_loop(0, depth, send_sums, 0, unroll=few)
         return carry
 
-    lax.fori_loop(0, depth, gather_unit, 0)
-    batch = min(32, owner_ref.shape[0])
-
-    def locate(step, carry):
-        rows = pl.ds(pl.multiple_of(step * SUBLANES, SUBLANES), SUBLANES)
-        source = source_ref[rows, :]
-        lane, tile = source % LANES, source // LANES
-
-        def look(group, found):
-            for t in range(batch):
-                row = group * batch + t
-                entry = jnp.broadcast_to(owner_ref[pl.ds(row, 1), :], (SUBLANES, LANES))
-                found = jnp.where(tile == row, gather_lanes(entry, lane), found)
-            return found
-
-        found = jnp.full((SUBLANES, LANES), -1, jnp.int32)
-        if owner_ref.shape[0] == batch:
-            found = look(0, found)
-        else:
-            found = lax.fori_loop(0, owner_ref.shape[0] // batch, look, found)
-        place_buf[rows, :] = found % LANES
-        return carry
-
-    lax.fori_loop(0, source_ref.shape[0] // SUBLANES, locate, 0)
-
-
+    def gather_turn(turn, carry):
+        await_meta(unit_of(turn * CORES)[0])
+        lax.fori_loop(turn * CORES, (turn + 1) * CORES, find_room, 0)
+        return lax.fori_loop(turn * CORES, (turn + 1) * CORES, gather_unit, carry)
+
+    def other_meta(turn, carry):
+        await_meta(level_at(turn * CORES + 1 - my_core))
+        return carry
+
+    lax.fori_loop(0, depth // CORES, gather_turn, 0)
+    lax.fori_loop(0, depth // CORES, other_meta, 0)
     at = {(0, 0): 0, (0, 1): 1, (0, 2): 2, (0, 3): 3, (0, 4): 4, (0, 5): 5, (5, 5): 6,
           (3, 5): 8, (1, 1): 9, (1, 2): 10, (1, 3): 11, (1, 4): 12, (1, 5): 13, (3, 3): 14, (3, 4): 15,
           (4, 4): 16, (4, 5): 17, (2, 2): 18, (2, 3): 19, (2, 4): 20, (2, 5): 21}
@@ -406,18 +437,20 @@
     def lead_fits():
         def fit_pair(step, carry):
             for core in range(CORES):
-                fit_level(step * CORES + core, CORES * (depth - (core == lead)))
+                fit_level(level_at(step * CORES + core), CORES * (depth - (core == lead)))
             return carry
 
         lax.fori_loop(0, depth // CORES, fit_pair, 0)
 
     def drain(ref, semaphore):
         pltpu.make_async_remote_copy(
-            src_ref=ref, dst_ref=ref, send_sem=semaphore, recv_sem=meta_recv_sem,
+            src_ref=ref, dst_ref=ref, send_sem=semaphore, recv_sem=meta_recv_sem.at[0],
             device_id=seat_coords(target(1)), device_id_type=MESH,
         ).wait_send()
 
-    def refit_level(level, tails):
+    def refit_level(turn, tails):
+        level = level_at(turn)
+
         def await_tables(count):
             pairs = pl.ds(0, count * CORES)
             pltpu.make_async_remote_copy(
@@ -544,11 +577,12 @@
             pltpu.SemaphoreType.DMA,
             pltpu.SemaphoreType.DMA((depth, 2)),
             pltpu.SemaphoreType.DMA,
-            pltpu.SemaphoreType.DMA,
+            pltpu.SemaphoreType.DMA((depth,)),
             pltpu.SemaphoreType.DMA,
             pltpu.SemaphoreType.DMA((depth,)),
             pltpu.SemaphoreType.DMA,
             pltpu.SemaphoreType.DMA((depth,)),
+            pltpu.SemaphoreType.REGULAR,
         ],
         compiler_params=pltpu.CompilerParams(
             collective_id=0, has_side_effects=True, vmem_limit_bytes=40 << 20

time: 21.2 us -> 21.2 us (level)
  no operation moved by 1% of the time
where the time goes in v7:
time: 21.2 us; the launch traced here: 21 us
  Pallas kernels  20.3 us (96%)
  between operations  0.64 us (3%)
    pallas_call x1, Pallas kernels, body(): pl.pallas_call(functools.partial(kernel, (groups, members, width, row_cou...  19.7 us
    pallas_call x1, Pallas kernels, body(): pl.pallas_call(release, out_shape=tuple((jax.ShapeDtypeStruct(r.shape, r....  0.66 us

profile of v7, /device:TPU:0, one launch (start us, length us, event | category | flops | bytes accessed | tf_op | source)
XLA Modules:
  0.0 21.0 jit_solution(6815777329877514417)
XLA Ops:
  0.6 19.7 %exchange_fit.1 = (f32[5,128]{1,0:T(8,128)S(1)}, f32[128,128]{1,0:T(8,128)S(1)}, f32[1,128]{1,0:T(1,128)S(1)}) custom-call(s32[128,128]{1,0:T(8,128)} %bitcast.9, s32[128,128]{1,0:T(8,128)} %bitcast.10, s32[32,128]{1,0:T(8,128)} %bitcast.13, s32[1,128]{1,0:T(1,128)} %bitcast.14, f32[5,16384]{1,0:T(8,128)} %partials_hbm.1, f32[128,128]{1,0:T(8,128)} %bitcast.11, ...), custom_call_target="tpu_custom_call" | custom-call | tf_op jit(solution)/shard_map/exchange_fit/pallas_call | solution.py:556
  20.3 0.7 %release.1 = (f32[5,128]{1,0:T(8,128)}, f32[128,128]{1,0:T(8,128)}, f32[1,128]{1,0:T(1,128)}) custom-call(f32[5,128]{1,0:T(8,128)S(1)} %get-tuple-element.9.a_ref, f32[128,128]{1,0:T(8,128)S(1)} %get-tuple-element.10.b_ref, f32[1,128]{1,0:T(1,128)S(1)} %get-tuple-element.11.c_ref), custom_call_target="tpu_custom_call" | custom-call | tf_op jit(solution)/shard_map/release/pallas_call | solution.py:593

commit v8 on v7

--- a/solution.py
+++ b/solution.py
@@ -218,7 +218,7 @@
         return carry
 
     lax.fori_loop(0, depth, send_meta_down, 0, unroll=few)
-    batches = ([0] + list(range(groups - 1, groups // 2, -1)), list(range(groups // 2, 0, -1)))
+    batches = ([0] + list(range(groups - 1, 1, -1)), [1])
 
     def send_rows(level):
         for core in range(CORES):

time: 21.2 us -> 21.2 us (level)
  no operation moved by 1% of the time
where the time goes in v8:
time: 21.2 us; the launch traced here: 21 us
  Pallas kernels  20.3 us (96%)
  between operations  0.64 us (3%)
    pallas_call x1, Pallas kernels, body(): pl.pallas_call(functools.partial(kernel, (groups, members, width, row_cou...  19.7 us
    pallas_call x1, Pallas kernels, body(): pl.pallas_call(release, out_shape=tuple((jax.ShapeDtypeStruct(r.shape, r....  0.66 us

profile of v8, /device:TPU:0, one launch (start us, length us, event | category | flops | bytes accessed | tf_op | source)
XLA Modules:
  0.0 21.0 jit_solution(3236926156960950167)
XLA Ops:
  0.6 19.7 %exchange_fit.1 = (f32[5,128]{1,0:T(8,128)S(1)}, f32[128,128]{1,0:T(8,128)S(1)}, f32[1,128]{1,0:T(1,128)S(1)}) custom-call(s32[128,128]{1,0:T(8,128)} %bitcast.9, s32[128,128]{1,0:T(8,128)} %bitcast.10, s32[32,128]{1,0:T(8,128)} %bitcast.13, s32[1,128]{1,0:T(1,128)} %bitcast.14, f32[5,16384]{1,0:T(8,128)} %partials_hbm.1, f32[128,128]{1,0:T(8,128)} %bitcast.11, ...), custom_call_target="tpu_custom_call" | custom-call | tf_op jit(solution)/shard_map/exchange_fit/pallas_call | solution.py:556
  20.3 0.7 %release.1 = (f32[5,128]{1,0:T(8,128)}, f32[128,128]{1,0:T(8,128)}, f32[1,128]{1,0:T(1,128)}) custom-call(f32[5,128]{1,0:T(8,128)S(1)} %get-tuple-element.9.a_ref, f32[128,128]{1,0:T(8,128)S(1)} %get-tuple-element.10.b_ref, f32[1,128]{1,0:T(1,128)S(1)} %get-tuple-element.11.c_ref), custom_call_target="tpu_custom_call" | custom-call | tf_op jit(solution)/shard_map/release/pallas_call | solution.py:593
